TPU v7x, 512 devices: a whole 4x4x16 slice. The times are simulated.
512 devices in a mesh: image: 4 (over y), crop: 8 (over x, core), proto: 16 (over z).
Axes of the slice: x: 4, y: 4, z: 16, core: 2. Of those that a mesh axis runs over, the one named last changes fastest.
Arguments:
- teacher_feats: bfloat16 [256, 2, 512], P('image'), may hold values from -4 to 4
- student_feats: bfloat16 [8, 256, 512], P('crop', 'image'), may hold values from -4 to 4
- teacher_protos: bfloat16 [512, 262144], P(None, ('crop', 'proto')), may hold values from -6 to 6
- student_protos: bfloat16 [512, 262144], P(None, ('crop', 'proto')), may hold values from -6 to 6
- pairing: int32 [8, 256], P('crop', 'image'), may hold values from 0 to 1
- row_weight: bfloat16 [8, 256], P('crop', 'image'), may hold values from 0.5 to 4
Outputs:
- feat_grad: float32 [8, 256, 512], P('crop', 'image')
- row_loss: float32 [8, 256], P('crop', 'image')
All inputs are finite; a program needn't handle non-finite values.
Results may differ from a plain program's by a relative error of at most 0.0016.
Values may be sent and summed in bfloat16 or wider, within the bound.
A program may use at most 64 MiB of HBM per device.

v0:
```python
import math

import jax
import jax.numpy as jnp
from jax import lax
from jax.sharding import Mesh
from jax.sharding import PartitionSpec as P

SWEEPS = 3
CROP_PROTO = ("crop_0", "crop_1", "proto")
CROP = ("crop_0", "crop_1")


epsilon = 1e-06
student_softness = 0.1
teacher_softness = 0.04


def sent_to_all(shard, axis):
    copies = jnp.broadcast_to(shard, (lax.axis_size(axis), *shard.shape))
    return lax.all_to_all(copies, axis, split_axis=0, concat_axis=0, tiled=True)


def taken_together(shard, axis):
    return sent_to_all(shard, axis).sum(axis=0)


def over_axes(shard, axes):
    far, near = axes
    return taken_together(taken_together(shard, near), far)


def joined_along(parts, dim):
    parts = jnp.moveaxis(parts, 0, dim)
    shape = parts.shape
    return parts.reshape(*shape[:dim], shape[dim] * shape[dim + 1], *shape[dim + 2 :])


def gather_directly(shard, axis, dim):
    return joined_along(sent_to_all(shard, axis), dim)


def split_up(shard, dim, length):
    before, after = (shard.shape[:dim], shard.shape[dim + 1 :])
    return jnp.moveaxis(shard.reshape(*before, length, -1, *after), dim, 0)


def summed_on_arrival(shard, axis, dim):
    length = lax.axis_size(axis)
    parts = lax.all_to_all(split_up(shard, dim, length), axis, 0, 0, tiled=True)
    return jnp.sum(parts.astype(jnp.float32), axis=0)


def sum_by_axis(shard, axes, dim):
    far, near = axes
    initial = summed_on_arrival(shard, far, dim)
    return summed_on_arrival(initial.astype(jnp.bfloat16), near, dim)


def side_by_side(arrays, axis, dim, along):
    widths = [math.prod(a.shape[along:]) for a in arrays]
    both = jnp.concatenate(
        [a.reshape(*a.shape[:along], w) for a, w in zip(arrays, widths)], axis=along
    )
    whole = sum_by_axis(both, axis, dim)
    parts = jnp.split(whole, [sum(widths[:k]) for k in range(1, len(widths))], axis=along)
    return tuple((b.reshape(*whole.shape[:along], *a.shape[along:]) for a, b in zip(arrays, parts)))


def in_one_piece(arrays, axis, dim, along):
    widths = [math.prod(a.shape[along:]) for a in arrays]
    both = jnp.concatenate(
        [a.reshape(*a.shape[:along], w) for a, w in zip(arrays, widths)], axis=along
    )
    whole = lax.all_gather(both, axis, axis=dim, tiled=True)
    parts = jnp.split(whole, [sum(widths[:k]) for k in range(1, len(widths))], axis=along)
    return tuple((b.reshape(*whole.shape[:along], *a.shape[along:]) for a, b in zip(arrays, parts)))


def unit_rows(raw_rows):
    return raw_rows * lax.rsqrt(jnp.sum(raw_rows * raw_rows, axis=-1, keepdims=True) + epsilon)


def unit_columns(weight_rows):
    entries = weight_rows.astype(jnp.float32)
    return (
        entries * lax.rsqrt(jnp.sum(entries * entries, axis=0, keepdims=True) + epsilon)
    ).astype(jnp.bfloat16)


def finish_rows(raw_rows, back_sum, cross_term, running_sums):
    scales = lax.rsqrt(jnp.sum(raw_rows * raw_rows, axis=-1, keepdims=True) + epsilon)
    along = jnp.sum(raw_rows * back_sum, axis=-1, keepdims=True)
    gradient = scales * back_sum - scales * scales * scales * raw_rows * along
    return (gradient, jnp.log(running_sums) - cross_term)


def column_step(transport_plan):
    return transport_plan / taken_together(jnp.sum(transport_plan, axis=0), "image")


def row_step(transport_plan):
    return (
        transport_plan
        / over_axes(jnp.sum(transport_plan, axis=1), ("crop_0", ("crop_1", "proto")))[:, None]
    )


def shards(teacher_feats, student_feats, teacher_protos, student_protos, pairing, row_weight):
    image_count = teacher_feats.shape[0]
    view_count = teacher_feats.shape[1]
    width = teacher_feats.shape[2]
    local_count = student_feats.shape[0]
    teacher_normalized_rows = (
        unit_rows(teacher_feats.astype(jnp.float32))
        .astype(jnp.bfloat16)
        .reshape(image_count * view_count, width)
    )
    teacher_weight_matrix = unit_columns(teacher_protos)
    student_weight_matrix = unit_columns(student_protos)
    features, picked, weight_rows = (
        gather_directly(student_feats, CROP, 0),
        gather_directly(pairing, CROP, 0),
        gather_directly(row_weight, CROP, 0),
    )
    student_normalized_rows = unit_rows(features.astype(jnp.float32)).astype(jnp.bfloat16)
    score_matrix = (
        jnp.einsum(
            "lbd,dk->lbk",
            student_normalized_rows,
            student_weight_matrix,
            preferred_element_type=jnp.float32,
        )
        / student_softness
    )
    exponent_terms = jnp.exp(score_matrix)
    partial_totals = jnp.sum(exponent_terms, axis=2)
    transport_plan = jnp.exp(
        jnp.dot(teacher_normalized_rows, teacher_weight_matrix, preferred_element_type=jnp.float32)
        / teacher_softness
    )
    running_sums = over_axes(partial_totals, ("crop_0", ("crop_1", "proto")))
    for sweep_index in range(SWEEPS):
        transport_plan = row_step(column_step(transport_plan))
    targets = transport_plan.astype(jnp.bfloat16).reshape(image_count, view_count, -1)
    selected_entries = jnp.zeros(score_matrix.shape, jnp.float32)
    for view_index in range(view_count):
        selected_entries = jnp.where(
            (picked == view_index)[:, :, None],
            targets[None, :, view_index, :].astype(jnp.float32),
            selected_entries,
        )
    cross_term = jnp.sum(selected_entries * score_matrix, axis=2)
    linear_factors = (
        weight_rows.astype(jnp.float32)[:, :, None]
        * (exponent_terms / running_sums[:, :, None] - selected_entries)
        / student_softness
    ).astype(jnp.bfloat16)
    back_sum = jnp.einsum(
        "lbk,dk->lbd", linear_factors, student_weight_matrix, preferred_element_type=jnp.float32
    )
    raw_rows = student_feats.astype(jnp.float32)
    row_count = local_count * image_count // lax.axis_size("proto")
    flat_back, flat_cross = side_by_side(
        (
            back_sum.reshape(-1, width).astype(jnp.bfloat16),
            cross_term.reshape(-1).astype(jnp.bfloat16),
        ),
        ("crop_0", ("crop_1", "proto")),
        0,
        1,
    )
    local_start = lax.axis_index("proto") * row_count
    own_raw = lax.dynamic_slice_in_dim(raw_rows.reshape(-1, width), local_start, row_count, 0)
    global_start = lax.axis_index(CROP) * local_count * image_count + local_start
    own_totals = lax.dynamic_slice_in_dim(running_sums.reshape(-1), global_start, row_count, 0)
    gradient, losses = finish_rows(own_raw, flat_back, flat_cross, own_totals)
    gradient, losses = in_one_piece((gradient, losses), "proto", 0, 1)
    return (
        gradient.reshape(local_count, image_count, width),
        losses.reshape(local_count, image_count),
    )


def solution(mesh):
    split = Mesh(
        mesh.devices.reshape(mesh.shape["image"], 4, 2, mesh.shape["proto"]),
        ("image", "crop_0", "crop_1", "proto"),
    )
    return jax.shard_map(
        shards,
        mesh=split,
        in_specs=(
            P("image", None, None),
            P(CROP, "image", None),
            P(None, CROP_PROTO),
            P(None, CROP_PROTO),
            P(CROP, "image"),
            P(CROP, "image"),
        ),
        out_specs=(P(CROP, "image", None), P(CROP, "image")),
        check_vma=False,
    )
```

profile of v0, /device:TPU:32, one launch (start us, length us, event | category | flops | bytes accessed | tf_op | source)
XLA Modules:
  0.0 250.6 jit_solution(4168137771601597833)
XLA Ops:
  0.6 1.1 fusion.32
  1.8 1.1 fusion.33
  2.9 2.0 fusion.2
  5.0 2.4 fusion.43
  7.4 9.7 %all_to_all.89 = f32[4,1,2048]{2,1,0:T(1,128)S(1)} all-to-all(f32[4,1,2048]{2,1,0:T(1,128)S(1)} %broadcast_in_dim.93), channel_id=1, replica_groups=mesh['image'=4,'crop_0'=4,'crop_1'=2,'proto'=16] {'image'}, dimensions={0} | all-to-all | bytes 65536 | tf_op jit(solution)/shard_map/all_to_all | solution.py:21
  17.4 26.2 %all_to_all.90 = f32[32,1,128]{2,1,0:T(1,128)S(1)} all-to-all(f32[32,1,128]{2,1,0:T(1,128)S(1)} %broadcast_in_dim.94), channel_id=1, replica_groups=mesh['image'=4,'crop_0'=4,'crop_1'=2,'proto'=16] {'crop_1','proto'}, dimensions={0} | all-to-all | bytes 32768 | tf_op jit(solution)/shard_map/all_to_all | solution.py:21
  43.6 9.4 %all_to_all.91 = f32[4,1,128]{2,1,0:T(1,128)S(1)} all-to-all(f32[4,1,128]{2,1,0:T(1,128)S(1)} %broadcast_in_dim.95), channel_id=1, replica_groups=mesh['image'=4,'crop_0'=4,'crop_1'=2,'proto'=16] {'crop_0'}, dimensions={0} | all-to-all | bytes 4096 | tf_op jit(solution)/shard_map/all_to_all | solution.py:21
  53.3 7.8 %all_to_all.92 = f32[4,1,2048]{2,1,0:T(1,128)S(1)} all-to-all(f32[4,1,2048]{2,1,0:T(1,128)S(1)} %broadcast_in_dim.96), channel_id=1, replica_groups=mesh['image'=4,'crop_0'=4,'crop_1'=2,'proto'=16] {'image'}, dimensions={0} | all-to-all | bytes 65536 | tf_op jit(solution)/shard_map/all_to_all | solution.py:21
  61.5 15.0 %all_to_all.93 = f32[32,1,128]{2,1,0:T(1,128)S(1)} all-to-all(f32[32,1,128]{2,1,0:T(1,128)S(1)} %broadcast_in_dim.97), channel_id=1, replica_groups=mesh['image'=4,'crop_0'=4,'crop_1'=2,'proto'=16] {'crop_1','proto'}, dimensions={0} | all-to-all | bytes 32768 | tf_op jit(solution)/shard_map/all_to_all | solution.py:21
  76.6 7.6 %all_to_all.94 = f32[4,1,128]{2,1,0:T(1,128)S(1)} all-to-all(f32[4,1,128]{2,1,0:T(1,128)S(1)} %broadcast_in_dim.98), channel_id=1, replica_groups=mesh['image'=4,'crop_0'=4,'crop_1'=2,'proto'=16] {'crop_0'}, dimensions={0} | all-to-all | bytes 4096 | tf_op jit(solution)/shard_map/all_to_all | solution.py:21
  84.6 7.8 %all_to_all.95 = f32[4,1,2048]{2,1,0:T(1,128)S(1)} all-to-all(f32[4,1,2048]{2,1,0:T(1,128)S(1)} %broadcast_in_dim.99), channel_id=1, replica_groups=mesh['image'=4,'crop_0'=4,'crop_1'=2,'proto'=16] {'image'}, dimensions={0} | all-to-all | bytes 65536 | tf_op jit(solution)/shard_map/all_to_all | solution.py:21
  93.4 4.8 %all-to-all-start.12 = ((f32[32,1,128]{2,1,0:T(1,128)}), f32[32,1,128]{2,1,0:T(1,128)S(1)}, u32[]{:S(2)}, u32[]{:S(2)}) async-start(f32[32,1,128]{2,1,0:T(1,128)} %broadcast_in_dim.100), calls=%async_computation.12 | async-start | bytes 32768 | tf_op jit(solution)/shard_map/all_to_all | solution.py:21
  98.7 10.5 %all-to-all-done.12 = f32[32,1,128]{2,1,0:T(1,128)S(1)} async-done(((f32[32,1,128]{2,1,0:T(1,128)}), f32[32,1,128]{2,1,0:T(1,128)S(1)}, u32[]{:S(2)}, u32[]{:S(2)}) %all-to-all-start.12) | async-done | bytes 16416 | tf_op jit(solution)/shard_map/all_to_all | solution.py:21
  109.9 3.3 %all-to-all-start.4 = ((s32[8,1,64]{2,1,0:T(1,128)}), s32[8,1,64]{2,1,0:T(1,128)S(1)}, u32[]{:S(2)}, u32[]{:S(2)}) async-start(s32[8,1,64]{2,1,0:T(1,128)} %broadcast_in_dim.91), calls=%async_computation.4 | async-start | bytes 8192 | tf_op jit(solution)/shard_map/all_to_all | solution.py:21
  113.2 5.1 %all-to-all-done.4 = s32[8,1,64]{2,1,0:T(1,128)S(1)} async-done(((s32[8,1,64]{2,1,0:T(1,128)}), s32[8,1,64]{2,1,0:T(1,128)S(1)}, u32[]{:S(2)}, u32[]{:S(2)}) %all-to-all-start.4) | async-done | bytes 2080 | tf_op jit(solution)/shard_map/all_to_all | solution.py:21
  118.9 3.2 %all-to-all-start.13 = ((f32[4,1,128]{2,1,0:T(1,128)}), f32[4,1,128]{2,1,0:T(1,128)S(1)}, u32[]{:S(2)}, u32[]{:S(2)}) async-start(f32[4,1,128]{2,1,0:T(1,128)} %broadcast_in_dim.101), calls=%async_computation.13 | async-start | bytes 4096 | tf_op jit(solution)/shard_map/all_to_all | solution.py:21
  122.1 5.2 %all-to-all-done.13 = f32[4,1,128]{2,1,0:T(1,128)S(1)} async-done(((f32[4,1,128]{2,1,0:T(1,128)}), f32[4,1,128]{2,1,0:T(1,128)S(1)}, u32[]{:S(2)}, u32[]{:S(2)}) %all-to-all-start.13) | async-done | bytes 2080 | tf_op jit(solution)/shard_map/all_to_all | solution.py:21
  127.3 0.8 broadcast_in_dim.88
  128.1 3.5 %all-to-all-start.1 = ((bf16[8,1,64,512]{3,2,1,0:T(8,128)(2,1)}), bf16[8,1,64,512]{3,2,1,0:T(8,128)(2,1)S(1)}, u32[]{:S(2)}, u32[]{:S(2)}) async-start(bf16[8,1,64,512]{3,2,1,0:T(8,128)(2,1)} %broadcast_in_dim.88), calls=%async_computation.1 | async-start | bytes 1048576 | tf_op jit(solution)/shard_map/all_to_all | solution.py:21
  133.2 1.2 fusion.34
  134.4 7.5 %all-to-all-done.1 = bf16[8,1,64,512]{3,2,1,0:T(8,128)(2,1)S(1)} async-done(((bf16[8,1,64,512]{3,2,1,0:T(8,128)(2,1)}), bf16[8,1,64,512]{3,2,1,0:T(8,128)(2,1)S(1)}, u32[]{:S(2)}, u32[]{:S(2)}) %all-to-all-start.1) | async-done | bytes 524320 | tf_op jit(solution)/shard_map/all_to_all | solution.py:21
  142.1 5.6 %exponential_reduce_fusion = (f32[8,64]{1,0:T(8,128)S(1)}, bf16[8,64]{1,0:T(8,128)(2,1)S(1)}, f32[8,64,2048]{2,1,0:T(8,128)}) fusion(f32[64,2048]{1,0:T(8,128)S(1)} %get-tuple-element.15, pred[8,64]{1,0:T(8,128)(4,1)S(1)} %get-tuple-element.9, f32[64,2048]{1,0:T(8,128)} %get-tuple-element.16, pred[8,64]{1,0:T(8,128)(4,1)S(1)} %get-tuple-element.8, ...), kind=kOutput, calls=%fused_computation.11 | convolution fusion | flops 1083964416 | bytes 7878656 | tf_op jit(solution)/shard_map/lbd,dk->lbk/dot_general | solution.py:128
  147.8 16.8 %all_to_all.96 = f32[32,1,512]{2,1,0:T(1,128)S(1)} all-to-all(f32[32,1,512]{2,1,0:T(1,128)S(1)} %reshape.190), channel_id=1, replica_groups=mesh['image'=4,'crop_0'=4,'crop_1'=2,'proto'=16] {'crop_1','proto'}, dimensions={0} | all-to-all | bytes 131072 | tf_op jit(solution)/shard_map/all_to_all | solution.py:21
  165.2 3.2 %all-to-all-start = ((bf16[8,1,64]{2,1,0:T(2,128)(2,1)}), bf16[8,1,64]{2,1,0:T(2,128)(2,1)S(1)}, u32[]{:S(2)}, u32[]{:S(2)}) async-start(bf16[8,1,64]{2,1,0:T(2,128)(2,1)} %broadcast_in_dim.87), calls=%async_computation | async-start | bytes 8192 | tf_op jit(solution)/shard_map/all_to_all | solution.py:21
  170.5 3.1 %all-to-all-done = bf16[8,1,64]{2,1,0:T(2,128)(2,1)S(1)} async-done(((bf16[8,1,64]{2,1,0:T(2,128)(2,1)}), bf16[8,1,64]{2,1,0:T(2,128)(2,1)S(1)}, u32[]{:S(2)}, u32[]{:S(2)}) %all-to-all-start) | async-done | bytes 1056 | tf_op jit(solution)/shard_map/all_to_all | solution.py:21
  173.6 3.4 %all-to-all-start.3 = ((f32[4,1,512]{2,1,0:T(1,128)}), f32[4,1,512]{2,1,0:T(1,128)S(1)}, u32[]{:S(2)}, u32[]{:S(2)}) async-start(f32[4,1,512]{2,1,0:T(1,128)} %reshape.192), calls=%async_computation.3 | async-start | bytes 16384 | tf_op jit(solution)/shard_map/all_to_all | solution.py:21
  177.1 5.0 %all-to-all-done.3 = f32[4,1,512]{2,1,0:T(1,128)S(1)} async-done(((f32[4,1,512]{2,1,0:T(1,128)}), f32[4,1,512]{2,1,0:T(1,128)S(1)}, u32[]{:S(2)}, u32[]{:S(2)}) %all-to-all-start.3) | async-done | bytes 8224 | tf_op jit(solution)/shard_map/all_to_all | solution.py:21
  182.9 4.2 %fusion.18 = bf16[8,64,512]{2,1,0:T(8,128)(2,1)S(1)} fusion(bf16[512,2048]{1,0:T(8,128)(2,1)S(1)} %copy-done.1, f32[2048]{0:T(1024)S(1)} %add_rsqrt_fusion.2, f32[8,64,2048]{2,1,0:T(8,128)} %get-tuple-element.14, f32[64,2048]{1,0:T(8,128)S(1)} %get-tuple-element.15, f32[64,2048]{1,0:T(8,128)} %get-tuple-element.16, f32[8,64]{1,0:T(8,128)S(1)} %reduce_sum.251, ...), kind=kOutput, calls=%fused_computation.28 | convolution fusion | flops 1085538304 | bytes 7877632 | tf_op jit(solution)/shard_map/lbk,dk->lbd/dot_general | solution.py:159
  187.5 10.9 %all_to_all.97 = bf16[4,128,513]{1,2,0:T(8,128)(2,1)S(1)} all-to-all(bf16[4,128,513]{1,2,0:T(8,128)(2,1)S(1)} %pad_maximum_fusion), channel_id=1, replica_groups=mesh['image'=4,'crop_0'=4,'crop_1'=2,'proto'=16] {'crop_0'}, dimensions={0} | all-to-all | bytes 1050624 | tf_op jit(solution)/shard_map/all_to_all | solution.py:50
  199.3 4.4 %all-to-all-start.15 = ((bf16[32,4,513]{2,1,0:T(4,128)(2,1)}), bf16[32,4,513]{2,1,0:T(4,128)(2,1)S(1)}, u32[]{:S(2)}, u32[]{:S(2)}) async-start(bf16[32,4,513]{2,1,0:T(4,128)(2,1)} %reshape.176), calls=%async_computation.15 | async-start | bytes 327680 | tf_op jit(solution)/shard_map/all_to_all | solution.py:50
  203.8 16.2 %all-to-all-done.15 = bf16[32,4,513]{2,1,0:T(4,128)(2,1)S(1)} async-done(((bf16[32,4,513]{2,1,0:T(4,128)(2,1)}), bf16[32,4,513]{2,1,0:T(4,128)(2,1)S(1)}, u32[]{:S(2)}, u32[]{:S(2)}) %all-to-all-start.15) | async-done | bytes 131360 | tf_op jit(solution)/shard_map/all_to_all | solution.py:50
  220.7 28.6 %all-gather = f32[16,4,513]{2,1,0:T(4,128)S(1)} all-gather(f32[1,4,513]{2,1,0:T(4,128)S(1)} %maximum_bitcast_fusion), channel_id=1, replica_groups=mesh['image'=4,'crop_0'=4,'crop_1'=2,'proto'=16] {'proto'}, dimensions={0}, use_global_device_ids=true | all-gather | bytes 139536 | tf_op jit(solution)/shard_map/all_gather | solution.py:75
  (76 shorter events, 12.9 us)
Async XLA Ops:
  5.0 93.3 %copy-start = (bf16[512,2048]{1,0:T(8,128)(2,1)S(1)}, bf16[512,2048]{1,0:T(8,128)(2,1)}, u32[]{:S(2)}) copy-start(bf16[512,2048]{1,0:T(8,128)(2,1)} %param.9) | copy-start | bytes 6291460
  7.4 101.9 %copy-start.3 = (s32[1,64]{1,0:T(1,128)S(1)}, s32[1,64]{1,0:T(1,128)}, u32[]{:S(2)}) copy-start(s32[1,64]{1,0:T(1,128)} %param.10) | copy-start | bytes 772
  7.4 119.9 %copy-start.2 = (bf16[1,64,512]{2,1,0:T(8,128)(2,1)S(1)}, bf16[1,64,512]{2,1,0:T(8,128)(2,1)}, u32[]{:S(2)}) copy-start(bf16[1,64,512]{2,1,0:T(8,128)(2,1)} %param.7) | copy-start | bytes 196612
  93.4 15.8 %all-to-all-start.12 = ((f32[32,1,128]{2,1,0:T(1,128)}), f32[32,1,128]{2,1,0:T(1,128)S(1)}, u32[]{:S(2)}, u32[]{:S(2)}) async-start(f32[32,1,128]{2,1,0:T(1,128)} %broadcast_in_dim.100), calls=%async_computation.12 | async-start | bytes 32768 | tf_op jit(solution)/shard_map/all_to_all | solution.py:21
  109.9 8.5 %all-to-all-start.4 = ((s32[8,1,64]{2,1,0:T(1,128)}), s32[8,1,64]{2,1,0:T(1,128)S(1)}, u32[]{:S(2)}, u32[]{:S(2)}) async-start(s32[8,1,64]{2,1,0:T(1,128)} %broadcast_in_dim.91), calls=%async_computation.4 | async-start | bytes 8192 | tf_op jit(solution)/shard_map/all_to_all | solution.py:21
  118.9 8.4 %all-to-all-start.13 = ((f32[4,1,128]{2,1,0:T(1,128)}), f32[4,1,128]{2,1,0:T(1,128)S(1)}, u32[]{:S(2)}, u32[]{:S(2)}) async-start(f32[4,1,128]{2,1,0:T(1,128)} %broadcast_in_dim.101), calls=%async_computation.13 | async-start | bytes 4096 | tf_op jit(solution)/shard_map/all_to_all | solution.py:21
  128.1 13.7 %all-to-all-start.1 = ((bf16[8,1,64,512]{3,2,1,0:T(8,128)(2,1)}), bf16[8,1,64,512]{3,2,1,0:T(8,128)(2,1)S(1)}, u32[]{:S(2)}, u32[]{:S(2)}) async-start(bf16[8,1,64,512]{3,2,1,0:T(8,128)(2,1)} %broadcast_in_dim.88), calls=%async_computation.1 | async-start | bytes 1048576 | tf_op jit(solution)/shard_map/all_to_all | solution.py:21
  142.1 22.5 %copy-start.4 = (bf16[1,64]{1,0:T(2,128)(2,1)S(1)}, bf16[1,64]{1,0:T(2,128)(2,1)}, u32[]{:S(2)}) copy-start(bf16[1,64]{1,0:T(2,128)(2,1)} %param.11) | copy-start | bytes 388
  142.1 40.8 %copy-start.1 = (bf16[512,2048]{1,0:T(8,128)(2,1)S(1)}, bf16[512,2048]{1,0:T(8,128)(2,1)}, u32[]{:S(2)}) copy-start(bf16[512,2048]{1,0:T(8,128)(2,1)} %param.9) | copy-start | bytes 6291460
  165.2 8.4 %all-to-all-start = ((bf16[8,1,64]{2,1,0:T(2,128)(2,1)}), bf16[8,1,64]{2,1,0:T(2,128)(2,1)S(1)}, u32[]{:S(2)}, u32[]{:S(2)}) async-start(bf16[8,1,64]{2,1,0:T(2,128)(2,1)} %broadcast_in_dim.87), calls=%async_computation | async-start | bytes 8192 | tf_op jit(solution)/shard_map/all_to_all | solution.py:21
  173.6 8.5 %all-to-all-start.3 = ((f32[4,1,512]{2,1,0:T(1,128)}), f32[4,1,512]{2,1,0:T(1,128)S(1)}, u32[]{:S(2)}, u32[]{:S(2)}) async-start(f32[4,1,512]{2,1,0:T(1,128)} %reshape.192), calls=%async_computation.3 | async-start | bytes 16384 | tf_op jit(solution)/shard_map/all_to_all | solution.py:21
  199.3 20.7 %all-to-all-start.15 = ((bf16[32,4,513]{2,1,0:T(4,128)(2,1)}), bf16[32,4,513]{2,1,0:T(4,128)(2,1)S(1)}, u32[]{:S(2)}, u32[]{:S(2)}) async-start(bf16[32,4,513]{2,1,0:T(4,128)(2,1)} %reshape.176), calls=%async_computation.15 | async-start | bytes 327680 | tf_op jit(solution)/shard_map/all_to_all | solution.py:50
where the time goes:
time: 252 us; the launch traced here: 251 us
  blocking collectives  140 us (56%)
  waiting for transfers between devices  52.6 us (21%)
  starting transfers between devices  25.9 us (10%)
  matrix products  12.2 us (5%)
  other arithmetic  10.3 us (4%)
  local copies, waits for them, and re-layouts  8.83 us (4%)
    all_to_all x8, blocking collectives, sent_to_all(): return lax.all_to_all(copies, axis, split_axis=0, concat_axis=0, tiled=True)  100 us
    all_to_all x6, waiting for transfers between devices, sent_to_all(): return lax.all_to_all(copies, axis, split_axis=0, concat_axis=0, tiled=True)  36.4 us
    all_gather x1, blocking collectives, in_one_piece(): whole = lax.all_gather(both, axis, axis=dim, tiled=True)  28.6 us
    all_to_all x6, starting transfers between devices, sent_to_all(): return lax.all_to_all(copies, axis, split_axis=0, concat_axis=0, tiled=True)  21.5 us
    all_to_all x1, waiting for transfers between devices, summed_on_arrival(): parts = lax.all_to_all(split_up(shard, dim, length), axis, 0, 0, tiled=True)  16.2 us
    all_to_all x1, blocking collectives, summed_on_arrival(): parts = lax.all_to_all(split_up(shard, dim, length), axis, 0, 0, tiled=True)  10.9 us
    dot_general x1, matrix products, shards(): jnp.einsum('lbd,dk->lbk', student_normalized_rows, student_weight_matrix,...  5.56 us
  transfers between devices with their start and end apart: 7, of which 7 were waited for; matrix products, arithmetic and copies ran while one was open for 2% of the time, Pallas kernels for 0%

commit v1 on v0

v1 whole, which is shorter than its diff:
```python
import functools

import jax
import jax.numpy as jnp
from jax import lax
from jax.experimental import pallas as pl
from jax.experimental.pallas import tpu as pltpu
from jax.sharding import PartitionSpec as P

EPSILON = 1e-06
MESH = pl.DeviceIdType.MESH
HIGHEST = lax.Precision.HIGHEST
F32 = jnp.float32
BF16 = jnp.bfloat16
NT = (((1,), (1,)), ((), ()))
ROWS = 512
COLS = 2048
LANES = 128
CHUNK = 256


def every(n, body):
    lax.fori_loop(0, n, lambda k, c: (body(k), c)[1], 0)


def unit_rows(x):
    return x * lax.rsqrt(jnp.sum(x * x, axis=1, keepdims=True) + EPSILON)


def unit_columns(raw, out):
    def chunk(j):
        cols = pl.ds(pl.multiple_of(j * LANES, LANES), LANES)
        w = raw[:, cols].astype(F32)
        scale = lax.rsqrt(jnp.sum(w * w, axis=0, keepdims=True) + EPSILON)
        out[:, cols] = (w * scale).astype(BF16)

    every(COLS // LANES, chunk)


def lane_sums(ref):
    ones = jnp.ones((8, LANES), F32)
    sums = lax.dot_general(ones, ref[...], NT, precision=HIGHEST, preferred_element_type=F32)
    return sums[0:1, :]


def kernel(
    y_n, c_n, z_n,
    tf_ref, sf_ref, pair_ref, weight_ref, tp_hbm, sp_hbm,
    grad_ref, loss_ref,
    tp, sp, wt, ws, t, e, tu, su, part, spart, ubuf, v, acc,
    r1p, r1z, r2p, r2z, a_out, a_in, az_out, az_in, a_all,
    ct_out, ct_in, cz_out, cz_in, c_tiles, ct_all, r3p, r3z,
    load, tu_s, tu_r, su_s, su_r, r1p_s, r1p_r, r1z_s, r1z_r, r2p_s, r2p_r, r2z_s, r2z_r,
    a_s, a_r, az_s, az_r, ag_s, ag_r, ct_s, ct_r, cz_s, cz_r, cg_s, cg_r, ca_s, ca_r,
    r3p_s, r3p_r, r3z_s, r3z_r,
):
    my_y, my_c, my_z = (lax.axis_index(a) for a in ("image", "crop", "proto"))

    def far_first(k):
        step = k + 1
        return z_n // 2 + (1 - 2 * lax.rem(step, 2)) * (step // 2)

    def push(src, dst, sends, recvs, axis, peer):
        pltpu.make_async_remote_copy(
            src_ref=src, dst_ref=dst, send_sem=sends, recv_sem=recvs,
            device_id={axis: peer}, device_id_type=MESH,
        ).start()

    def to_crops(src, dst, sends, recvs):
        def one(k):
            peer = lax.rem(my_c + k + 1, c_n)
            push(src(peer), dst, sends, recvs, "crop", peer)

        every(c_n - 1, one)

    def to_protos(src, dst, sends, recvs):
        def one(k):
            peer = lax.rem(my_z + far_first(k), z_n)
            push(src(peer), dst, sends, recvs, "proto", peer)

        every(z_n - 1, one)

    def await_bytes(ref, n, sem):
        some = ref.at[pl.ds(0, n)]
        pltpu.make_async_copy(some, some, sem).wait()

    loads = [
        pltpu.make_async_copy(tp_hbm, tp, load.at[0]),
        pltpu.make_async_copy(sp_hbm, sp, load.at[1]),
    ]
    for copy in loads:
        copy.start()

    barrier = pltpu.get_barrier_semaphore()

    def greet(axis, me, n):
        def one(k):
            pl.semaphore_signal(
                barrier, inc=1, device_id={axis: lax.rem(me + k + 1, n)}, device_id_type=MESH
            )

        every(n - 1, one)

    greet("proto", my_z, z_n)
    greet("crop", my_c, c_n)
    greet("image", my_y, y_n)

    tu[my_y] = unit_rows(tf_ref[...].astype(F32)).astype(BF16)
    su[my_c] = unit_rows(sf_ref[...].astype(F32)).astype(BF16)

    pl.semaphore_wait(barrier, y_n + c_n + z_n - 3)

    def give_rows(k):
        peer = lax.rem(my_y + k + 1, y_n)
        push(tu.at[my_y], tu.at[my_y], tu_s, tu_r, "image", peer)

    every(y_n - 1, give_rows)
    to_crops(lambda peer: su.at[my_c], su.at[my_c], su_s, su_r)

    loads[0].wait()
    unit_columns(tp, wt)
    await_bytes(tu, y_n - 1, tu_r)

    def transport(j):
        cols = pl.ds(pl.multiple_of(j * CHUNK, CHUNK), CHUNK)
        rows = tu[...].reshape(ROWS, ROWS)
        entries = jnp.exp(jnp.dot(rows, wt[:, cols], preferred_element_type=F32) * 25.0)
        t[:, cols] = entries
        v[:, cols] = jnp.broadcast_to(1.0 / jnp.sum(entries, axis=0, keepdims=True), (8, CHUNK))

    every(COLS // CHUNK, transport)

    def row_pass():
        def block(r, carry):
            rows = pl.ds(pl.multiple_of(r * 8, 8), 8)
            total = t[rows, 0:LANES] * v[:, 0:LANES]
            for k in range(1, COLS // LANES):
                cols = slice(k * LANES, (k + 1) * LANES)
                total = total + t[rows, cols] * v[:, cols]
            part[rows, :] = total
            return carry

        lax.fori_loop(0, ROWS // 8, block, 0, unroll=4)
        return lane_sums(part)

    def column_pass(row_sums):
        u = 1.0 / row_sums
        for q in range(ROWS // LANES):
            piece = u[:, q * LANES : (q + 1) * LANES]
            ubuf[q * LANES : (q + 1) * LANES, :] = jnp.broadcast_to(piece, (LANES, LANES)).T

        def block(r, sums):
            rows = pl.ds(pl.multiple_of(r * 8, 8), 8)
            scale = ubuf[rows, :]
            return tuple(
                s + t[rows, k * LANES : (k + 1) * LANES] * scale for k, s in enumerate(sums)
            )

        zero = tuple(jnp.zeros((8, LANES), F32) for _ in range(COLS // LANES))
        sums = lax.fori_loop(0, ROWS // 8, block, zero, unroll=4)
        for k, s in enumerate(sums):
            v[:, k * LANES : (k + 1) * LANES] = jnp.broadcast_to(
                1.0 / jnp.sum(s, axis=0, keepdims=True), (8, LANES)
            )

    r1p[my_c] = row_pass()
    to_crops(lambda peer: r1p.at[my_c], r1p.at[my_c], r1p_s, r1p_r)

    loads[1].wait()
    unit_columns(sp, ws)

    await_bytes(r1p, c_n - 1, r1p_r)
    r1z[my_z] = jnp.sum(r1p[...], axis=0)
    to_protos(lambda peer: r1z.at[my_z], r1z.at[my_z], r1z_s, r1z_r)

    await_bytes(su, c_n - 1, su_r)
    spart[...] = jnp.zeros_like(spart)

    def student(j):
        cols = pl.ds(pl.multiple_of(j * CHUNK, CHUNK), CHUNK)
        rows = su[...].reshape(ROWS, ROWS)
        terms = jnp.exp(jnp.dot(rows, ws[:, cols], preferred_element_type=F32) * 10.0)
        spart[...] += terms[:, :LANES] + terms[:, LANES:]
        e[:, cols] = terms.astype(BF16)

    every(COLS // CHUNK, student)

    def student_back(j):
        some = pl.ds(pl.multiple_of(j * CHUNK, CHUNK), CHUNK)
        acc[...] = lax.dot_general(e[...], ws[some, :], NT, preferred_element_type=F32)
        a_out[:, :, some] = acc[...].astype(BF16).reshape(c_n, ROWS // c_n, CHUNK)

    every(ROWS // CHUNK, student_back)
    to_crops(lambda peer: a_out.at[peer], a_in.at[my_c], a_s, a_r)
    partial_totals = lane_sums(spart)

    await_bytes(r1z, z_n - 1, r1z_r)
    column_pass(jnp.sum(r1z[...], axis=0))
    r2p[my_c] = jnp.concatenate([row_pass(), partial_totals], axis=1)
    to_crops(lambda peer: r2p.at[my_c], r2p.at[my_c], r2p_s, r2p_r)
    await_bytes(r2p, c_n - 1, r2p_r)
    r2z[my_z] = jnp.sum(r2p[...], axis=0)
    to_protos(lambda peer: r2z.at[my_z], r2z.at[my_z], r2z_s, r2z_r)

    await_bytes(a_in, c_n - 1, a_r)
    a_in[my_c] = a_out[my_c]
    for g in range(8):
        rows = slice(g * 8, g * 8 + 8)
        total = a_in[0, rows, :].astype(F32)
        for k in range(1, c_n):
            total = total + a_in[k, rows, :].astype(F32)
        for h in range(2):
            az_out[2 * g + h] = total[:, h * 256 : (h + 1) * 256].astype(BF16)
    to_protos(lambda peer: az_out.at[peer], az_in.at[my_z], az_s, az_r)

    await_bytes(r2z, z_n - 1, r2z_r)
    second = jnp.sum(r2z[...], axis=0)
    totals = second[:, ROWS:]
    column_pass(second[:, :ROWS])

    own_rows = pl.ds(pl.multiple_of(my_y * LANES, LANES), LANES)
    for k in range(COLS // CHUNK):
        cols = slice(k * CHUNK, (k + 1) * CHUNK)
        scaled = t[own_rows, cols] * v[0:1, cols]
        e[0:LANES, cols] = scaled.astype(BF16)
        halves = scaled[:, :LANES] + scaled[:, LANES:]
        part[0:LANES, :] = halves if k == 0 else part[0:LANES, :] + halves
    r3p[my_c] = lane_sums(part.at[0:LANES])
    sums = lax.dot_general(e[0:LANES, :], ws[...], NT, preferred_element_type=F32)
    ct_out[...] = sums.astype(BF16).reshape(c_n, 16, ROWS)
    to_crops(lambda peer: ct_out.at[peer], ct_in.at[my_c], ct_s, ct_r)
    to_crops(lambda peer: r3p.at[my_c], r3p.at[my_c], r3p_s, r3p_r)
    ct_in[my_c] = ct_out[my_c]
    await_bytes(ct_in, c_n - 1, ct_r)
    await_bytes(r3p, c_n - 1, r3p_r)
    total = jnp.sum(ct_in[...].astype(F32), axis=0)
    for g in range(2):
        for k in range(4):
            tile = total[g * 8 : g * 8 + 8, k * LANES : (k + 1) * LANES]
            cz_out[4 * g + k] = tile.astype(BF16)
    r3z[my_z] = jnp.sum(r3p[...], axis=0)
    to_protos(lambda peer: cz_out.at[lax.rem(peer, 8)], cz_in.at[my_z], cz_s, cz_r)
    to_protos(lambda peer: r3z.at[my_z], r3z.at[my_z], r3z_s, r3z_r)
    cz_in[my_z] = cz_out[lax.rem(my_z, 8)]

    await_bytes(az_in, z_n - 1, az_r)
    az_in[my_z] = az_out[my_z]
    a_all[my_z] = jnp.sum(az_in[...].astype(F32), axis=0)
    to_protos(lambda peer: a_all.at[my_z], a_all.at[my_z], ag_s, ag_r)

    await_bytes(cz_in, z_n - 1, cz_r)
    mine = lax.rem(my_z, 8)
    c_tiles[mine] = jnp.sum(cz_in[...].astype(F32), axis=0)

    def near(k):
        offset = k + z_n - 4 + jnp.where(k >= 4, 1, 0)
        peer = lax.rem(my_z + offset, z_n)
        push(c_tiles.at[mine], c_tiles.at[mine], cg_s, cg_r, "proto", peer)

    every(7, near)
    await_bytes(c_tiles, 7, cg_r)
    ct_all[my_c] = c_tiles[...]
    to_crops(lambda peer: c_tiles, ct_all.at[my_c], ca_s, ca_r)

    await_bytes(r3z, z_n - 1, r3z_r)
    last = 1.0 / jnp.sum(r3z[...], axis=0)
    await_bytes(a_all, z_n - 1, ag_r)

    images = ROWS // c_n
    lane = lax.broadcasted_iota(jnp.int32, (images, ROWS), 1)
    row = lax.broadcasted_iota(jnp.int32, (images, ROWS), 0)

    def as_column(values, first):
        wide = jnp.broadcast_to(values, (images, values.shape[1]))
        n = values.shape[1]
        picked = jnp.where(lane[:, :n] == row[:, :n] + first, wide, jnp.zeros_like(wide))
        return jnp.sum(picked, axis=1, keepdims=True)

    view = as_column(pair_ref[...].astype(F32), 0) > 0.5
    weight = as_column(weight_ref[...].astype(F32), 0)
    total_column = as_column(totals, my_c * images)
    scale_0 = as_column(last, 0)
    scale_1 = as_column(last, images)
    x = sf_ref[...].astype(F32)
    unit = su[my_c].astype(F32)
    norm = lax.rsqrt(jnp.sum(x * x, axis=1, keepdims=True) + EPSILON)
    log_total = jnp.log(total_column)
    first = jnp.concatenate(
        [jnp.concatenate([a_all[2 * g], a_all[2 * g + 1]], axis=1) for g in range(8)], axis=0
    ) / total_column

    await_bytes(ct_all, c_n - 1, ca_r)

    def summed(view_index):
        blocks = []
        for g in range(8):
            c, h = 4 * view_index + g // 2, g % 2
            blocks.append(jnp.concatenate([ct_all[c, 4 * h + k] for k in range(4)], axis=1))
        return jnp.concatenate(blocks, axis=0)

    chosen = jnp.where(view, summed(1) * scale_1, summed(0) * scale_0)
    back = (weight * 10.0) * (first - chosen)
    cross = jnp.sum(unit * chosen, axis=1, keepdims=True) * 10.0
    along = jnp.sum(x * back, axis=1, keepdims=True)
    grad_ref[...] = norm * back - norm * norm * norm * x * along
    losses = jnp.broadcast_to(log_total - cross, (images, images))
    eye = lane[:, :images] == row[:, :images]
    loss_ref[...] = jnp.sum(jnp.where(eye, losses, 0.0), axis=0, keepdims=True)

    for ref, n, sem in (
        (tu, y_n - 1, tu_s), (su, c_n - 1, su_s), (r1p, c_n - 1, r1p_s), (r1z, z_n - 1, r1z_s),
        (r2p, c_n - 1, r2p_s), (r2z, z_n - 1, r2z_s), (a_in, c_n - 1, a_s),
        (az_in, z_n - 1, az_s), (a_all, z_n - 1, ag_s), (ct_in, c_n - 1, ct_s),
        (cz_in, z_n - 1, cz_s), (c_tiles, 7, cg_s), (ct_all, c_n - 1, ca_s),
        (r3p, c_n - 1, r3p_s), (r3z, z_n - 1, r3z_s),
    ):
        await_bytes(ref, n, sem)


def solution(mesh):
    y_n, c_n, z_n = (mesh.shape[a] for a in ("image", "crop", "proto"))

    def step(teacher_feats, student_feats, teacher_protos, student_protos, pairing, row_weight):
        images, views, width = teacher_feats.shape
        teacher = jnp.transpose(teacher_feats, (1, 0, 2)).reshape(views * images, width)
        vmem = pl.BlockSpec(memory_space=pltpu.VMEM)
        hbm = pl.BlockSpec(memory_space=pl.ANY)
        dma = pltpu.SemaphoreType.DMA
        grad, loss = pl.pallas_call(
            functools.partial(kernel, y_n, c_n, z_n),
            out_shape=(
                jax.ShapeDtypeStruct((images, width), F32),
                jax.ShapeDtypeStruct((1, images), F32),
            ),
            in_specs=[vmem] * 4 + [hbm] * 2,
            out_specs=(vmem, vmem),
            scratch_shapes=[
                pltpu.VMEM((width, COLS), BF16),
                pltpu.VMEM((width, COLS), BF16),
                pltpu.VMEM((width, COLS), BF16),
                pltpu.VMEM((width, COLS), BF16),
                pltpu.VMEM((ROWS, COLS), F32),
                pltpu.VMEM((ROWS, COLS), BF16),
                pltpu.VMEM((y_n, views * images, width), BF16),
                pltpu.VMEM((c_n, images, width), BF16),
                pltpu.VMEM((ROWS, LANES), F32),
                pltpu.VMEM((ROWS, LANES), F32),
                pltpu.VMEM((ROWS, LANES), F32),
                pltpu.VMEM((8, COLS), F32),
                pltpu.VMEM((ROWS, CHUNK), F32),
                pltpu.VMEM((c_n, 1, ROWS), F32),
                pltpu.VMEM((z_n, 1, ROWS), F32),
                pltpu.VMEM((c_n, 1, 2 * ROWS), F32),
                pltpu.VMEM((z_n, 1, 2 * ROWS), F32),
                pltpu.VMEM((c_n, images, width), BF16),
                pltpu.VMEM((c_n, images, width), BF16),
                pltpu.VMEM((z_n, 8, 256), BF16),
                pltpu.VMEM((z_n, 8, 256), BF16),
                pltpu.VMEM((z_n, 8, 256), F32),
                pltpu.VMEM((c_n, 16, width), BF16),
                pltpu.VMEM((c_n, 16, width), BF16),
                pltpu.VMEM((8, 8, LANES), BF16),
                pltpu.VMEM((z_n, 8, LANES), BF16),
                pltpu.VMEM((8, 8, LANES), F32),
                pltpu.VMEM((c_n, 8, 8, LANES), F32),
                pltpu.VMEM((c_n, 1, LANES), F32),
                pltpu.VMEM((z_n, 1, LANES), F32),
                dma((2,)),
            ]
            + [dma(())] * 30,
            compiler_params=pltpu.CompilerParams(collective_id=0, has_side_effects=True),
        )(
            teacher,
            student_feats.reshape(images, width),
            pairing,
            row_weight,
            teacher_protos,
            student_protos,
        )
        return grad.reshape(1, images, width), loss

    return jax.shard_map(
        step,
        mesh=mesh,
        in_specs=(
            P("image", None, None),
            P("crop", "image", None),
            P(None, ("crop", "proto")),
            P(None, ("crop", "proto")),
            P("crop", "image"),
            P("crop", "image"),
        ),
        out_specs=(P("crop", "image", None), P("crop", "image")),
        check_vma=False,
    )
```

time: 252 us -> 82.3 us (0.33)
  the two profiles are of different devices: /device:TPU:32 before, /device:TPU:1 now
where the time goes in v1:
time: 82.3 us; the launch traced here: 82.2 us
  Pallas kernels  77.2 us (94%)
  local copies, waits for them, and re-layouts  4.32 us (5%)
    pallas_call x1, Pallas kernels, step(): pl.pallas_call(functools.partial(kernel, y_n, c_n, z_n), out_shape=(jax.S...  77.2 us
    unnamed x2, local copies, waits for them, and re-layouts  2.74 us

profile of v1, /device:TPU:1, one launch (start us, length us, event | category | flops | bytes accessed | tf_op | source)
XLA Modules:
  0.0 82.2 jit_solution(15778052311842205745)
XLA Ops:
  0.6 1.6 %copy.8 = bf16[2,64,512]{2,1,0:T(8,128)(2,1)} copy(bf16[2,64,512]{2,0,1:T(2,128)(2,1)} %bitcast.5) | data formatting | bytes 262144 | tf_op jit(solution)/shard_map/transpose | solution.py:325
  2.2 77.2 %shard_map.77 = (f32[64,512]{1,0:T(8,128)}, f32[1,64]{1,0:T(1,128)}) custom-call(bf16[128,512]{1,0:T(8,128)(2,1)} %bitcast.4, bf16[64,512]{1,0:T(8,128)(2,1)} %bitcast.7, s32[1,64]{1,0:T(1,128)} %pair_ref.1, bf16[1,64]{1,0:T(2,128)(2,1)} %weight_ref.1, bf16[512,2048]{1,0:T(8,128)(2,1)} %tp_hbm.1, bf16[512,2048]{1,0:T(8,128)(2,1)} %sp_hbm.1), custom_call_target="tpu_custom_call" | custom-call | tf_op jit(solution)/shard_map/pallas_call | solution.py:329
  79.4 1.6 %copy.11 = f32[1,64,512]{2,1,0:T(8,128)} copy(f32[1,64,512]{2,1,0:T(8,128)} %bitcast.6) | data formatting | bytes 262144
  81.0 1.2 %copy.12 = f32[1,64]{1,0:T(1,128)} copy(f32[1,64]{1,0:T(1,128)} %get-tuple-element.9) | data formatting | bytes 512

commit v2 on v1

v2 whole, which is shorter than its diff:
```python
import functools

import jax
import jax.numpy as jnp
from jax import lax
from jax.experimental import pallas as pl
from jax.experimental.pallas import tpu as pltpu
from jax.sharding import PartitionSpec as P

EPSILON = 1e-06
MESH = pl.DeviceIdType.MESH
F32 = jnp.float32
BF16 = jnp.bfloat16
NT = (((1,), (1,)), ((), ()))
ROWS = 512
COLS = 2048
LANES = 128
CHUNK = 256


def every(n, body):
    lax.fori_loop(0, n, lambda k, c: (body(k), c)[1], 0)


def unit_rows(x):
    return x * lax.rsqrt(jnp.sum(x * x, axis=1, keepdims=True) + EPSILON)


def unit_columns(raw, out):
    def chunk(j):
        cols = pl.ds(pl.multiple_of(j * LANES, LANES), LANES)
        w = raw[:, cols].astype(F32)
        scale = lax.rsqrt(jnp.sum(w * w, axis=0, keepdims=True) + EPSILON)
        out[:, cols] = (w * scale).astype(BF16)

    every(COLS // LANES, chunk)


def lane_sums(ref, groups):
    sums = [
        jnp.sum(ref[q * LANES : (q + 1) * LANES, :].T, axis=0, keepdims=True) for q in range(groups)
    ]
    return jnp.concatenate(sums, axis=0) if groups > 1 else sums[0]


def kernel(
    y_n, c_n, z_n,
    tf_hbm, sf_hbm, pair_hbm, weight_hbm, tp_hbm, sp_hbm,
    grad_ref, loss_ref,
    tf, sf, pair, weight, tp, sp, wt, ws, t, e, tu, su, part, spart, ubuf, v, csum,
    r1p, r1z, r2p, r2z, tot_p, tot_sum, tot_z, pairs,
    a_out, a_in, az_out, az_in, a_all,
    ct_out, ct_in, cz_out, cz_in, c_tiles, pick_out, pick_in, r3p, r3z,
    load, tu_r, th_r,
    tu_s, th_s, su_s, su_r, sh_s, sh_r, pr_s, pr_r, r1p_s, r1p_r, r1z_s, r1z_r,
    r2p_s, r2p_r, r2z_s, r2z_r, tp_s, tp_r, tz_s, tz_r, a_s, a_r, az_s, az_r, ag_s, ag_r,
    ct_s, ct_r, cz_s, cz_r, cg_s, cg_r, ca_s, ca_r, r3p_s, r3p_r, r3z_s, r3z_r,
):
    my_y, my_c, my_z = (lax.axis_index(a) for a in ("image", "crop", "proto"))
    side = lax.rem(my_c, 2)
    partner = my_c + 1 - 2 * side

    loads = [
        pltpu.make_async_copy(src, dst, load.at[k])
        for k, (src, dst) in enumerate(
            ((tf_hbm, tf), (sf_hbm, sf), (tp_hbm, tp), (sp_hbm, sp), (pair_hbm, pair), (weight_hbm, weight))
        )
    ]
    for copy in loads:
        copy.start()

    def far_first(k):
        step = k + 1
        return z_n // 2 + (1 - 2 * lax.rem(step, 2)) * (step // 2)

    def push(src, dst, sends, recvs, axis, peer):
        pltpu.make_async_remote_copy(
            src_ref=src, dst_ref=dst, send_sem=sends, recv_sem=recvs,
            device_id={axis: peer}, device_id_type=MESH,
        ).start()

    def to_crops(src, dst, sends, recvs):
        def one(k):
            peer = lax.rem(my_c + k + 1, c_n)
            push(src(peer), dst, sends, recvs, "crop", peer)

        every(c_n - 1, one)

    def to_protos(src, dst, sends, recvs):
        def one(k):
            peer = lax.rem(my_z + far_first(k), z_n)
            push(src(peer), dst, sends, recvs, "proto", peer)

        every(z_n - 1, one)

    def await_bytes(ref, n, sem):
        some = ref.at[pl.ds(0, n)]
        pltpu.make_async_copy(some, some, sem).wait()

    barrier = pltpu.get_barrier_semaphore()

    def greet(axis, me, n):
        def one(k):
            pl.semaphore_signal(
                barrier, inc=1, device_id={axis: lax.rem(me + k + 1, n)}, device_id_type=MESH
            )

        every(n - 1, one)

    greet("proto", my_z, z_n)
    greet("image", my_y, y_n)
    greet("crop", my_c, c_n)

    loads[0].wait()
    for g in range(2):
        tu[my_y, g] = unit_rows(tf[:, g, :].astype(F32)).astype(BF16)
    loads[1].wait()
    su[my_c] = unit_rows(sf[...].astype(F32)).astype(BF16)
    loads[4].wait()
    pairs[my_c] = pair[...].astype(F32)
    loads[2].wait()
    unit_columns(tp, wt)

    pl.semaphore_wait(barrier, y_n + c_n + z_n - 3)

    def give_rows(k):
        peer = lax.rem(my_y + 2 * k + 1 - 3 * (k // 2), y_n)
        push(tu.at[my_y, side], tu.at[my_y, side], tu_s, tu_r.at[my_y], "image", peer)

    every(y_n - 1, give_rows)

    def give_students(k):
        peer = lax.rem(my_c + 2 * k + 2, c_n)
        push(su.at[my_c], su.at[my_c], su_s, su_r, "crop", peer)

    every(c_n // 2 - 1, give_students)
    push(su.at[my_c], su.at[my_c], sh_s, sh_r, "crop", partner)
    to_crops(lambda peer: pairs.at[my_c], pairs.at[my_c], pr_s, pr_r)

    def transport(y, first):
        def chunk(j):
            cols = pl.ds(pl.multiple_of(j * CHUNK, CHUNK), CHUNK)
            rows = tu[y].reshape(LANES, ROWS)
            terms = jnp.exp(jnp.dot(rows, wt[:, cols], preferred_element_type=F32) * 25.0)
            t[pl.ds(pl.multiple_of(y * LANES, LANES), LANES), cols] = terms
            sums = jnp.sum(terms.reshape(LANES // 8, 8, CHUNK), axis=0)
            csum[:, cols] = sums if first else csum[:, cols] + sums

        every(COLS // CHUNK, chunk)

    def hand_over(y):
        pltpu.make_async_copy(tu.at[y, side], tu.at[y, side], tu_r.at[y]).wait()
        push(tu.at[y, side], tu.at[y, side], th_s, th_r.at[y], "crop", partner)

    def handed(y):
        pltpu.make_async_copy(tu.at[y, side], tu.at[y, side], th_r.at[y]).wait()

    others = [lax.rem(my_y + k, y_n) for k in (1, 3, 2)]
    transport(my_y, True)
    loads[3].wait()
    unit_columns(sp, ws)
    hand_over(others[0])
    hand_over(others[1])
    handed(others[0])
    transport(others[0], False)
    hand_over(others[2])
    handed(others[1])
    transport(others[1], False)
    handed(others[2])
    transport(others[2], False)

    def set_v(sums):
        for k, s in enumerate(sums):
            v[:, k * LANES : (k + 1) * LANES] = jnp.broadcast_to(
                1.0 / jnp.sum(s, axis=0, keepdims=True), (8, LANES)
            )

    set_v([csum[:, k * LANES : (k + 1) * LANES] for k in range(COLS // LANES)])

    def row_pass():
        def block(r, carry):
            rows = pl.ds(pl.multiple_of(r * 8, 8), 8)
            total = t[rows, 0:LANES] * v[:, 0:LANES]
            for k in range(1, COLS // LANES):
                cols = slice(k * LANES, (k + 1) * LANES)
                total = total + t[rows, cols] * v[:, cols]
            part[rows, :] = total
            return carry

        lax.fori_loop(0, ROWS // 8, block, 0, unroll=4)
        return lane_sums(part, 4)

    def column_pass(row_sums):
        u = 1.0 / row_sums
        for q in range(ROWS // LANES):
            ubuf[q * LANES : (q + 1) * LANES, :] = jnp.broadcast_to(u[q : q + 1, :], (LANES, LANES)).T

        def block(r, sums):
            rows = pl.ds(pl.multiple_of(r * 8, 8), 8)
            scale = ubuf[rows, :]
            return tuple(
                s + t[rows, k * LANES : (k + 1) * LANES] * scale for k, s in enumerate(sums)
            )

        zero = tuple(jnp.zeros((8, LANES), F32) for _ in range(COLS // LANES))
        set_v(lax.fori_loop(0, ROWS // 8, block, zero, unroll=4))

    r1p[my_c] = row_pass()
    to_crops(lambda peer: r1p.at[my_c], r1p.at[my_c], r1p_s, r1p_r)

    await_bytes(su, c_n // 2 - 1, su_r)

    def hand_students(k):
        slot = lax.rem(my_c + 2 * k + 2, c_n)
        push(su.at[slot], su.at[slot], sh_s, sh_r, "crop", partner)

    every(c_n // 2 - 1, hand_students)
    await_bytes(su, c_n // 2, sh_r)
    spart[...] = jnp.zeros_like(spart)

    def student(j):
        cols = pl.ds(pl.multiple_of(j * CHUNK, CHUNK), CHUNK)
        rows = su[...].reshape(ROWS, ROWS)
        terms = jnp.exp(jnp.dot(rows, ws[:, cols], preferred_element_type=F32) * 10.0)
        spart[...] += terms[:, :LANES] + terms[:, LANES:]
        e[:, cols] = terms.astype(BF16)

    every(COLS // CHUNK, student)

    await_bytes(r1p, c_n - 1, r1p_r)
    r1z[my_z] = jnp.sum(r1p[...], axis=0).astype(BF16)
    to_protos(lambda peer: r1z.at[my_z], r1z.at[my_z], r1z_s, r1z_r)

    for j in range(2):
        some = slice(j * CHUNK, (j + 1) * CHUNK)
        back = lax.dot_general(e[...], ws[some, :], NT, preferred_element_type=F32)
        a_out[:, :, some] = back.astype(BF16).reshape(c_n, ROWS // c_n, CHUNK)
    to_crops(lambda peer: a_out.at[peer], a_in.at[my_c], a_s, a_r)
    tot_p[my_c] = lane_sums(spart, 4)
    to_crops(lambda peer: tot_p.at[my_c], tot_p.at[my_c], tp_s, tp_r)

    await_bytes(r1z, z_n - 1, r1z_r)
    column_pass(jnp.sum(r1z[...].astype(F32), axis=0))
    r2p[my_c] = row_pass()
    to_crops(lambda peer: r2p.at[my_c], r2p.at[my_c], r2p_s, r2p_r)

    await_bytes(a_in, c_n - 1, a_r)
    a_in[my_c] = a_out[my_c]
    for g in range(8):
        rows = slice(g * 8, g * 8 + 8)
        total = a_in[0, rows, :].astype(F32)
        for k in range(1, c_n):
            total = total + a_in[k, rows, :].astype(F32)
        for h in range(2):
            az_out[2 * g + h] = total[:, h * 256 : (h + 1) * 256].astype(BF16)
    await_bytes(tot_p, c_n - 1, tp_r)
    whole = jnp.sum(tot_p[...], axis=0)
    for q in range(4):
        tot_sum[q] = whole[q : q + 1, :]
    tot_z[my_z] = tot_sum[my_c // 2]

    await_bytes(r2p, c_n - 1, r2p_r)
    r2z[my_z] = jnp.sum(r2p[...], axis=0).astype(BF16)
    to_protos(lambda peer: r2z.at[my_z], r2z.at[my_z], r2z_s, r2z_r)
    to_protos(lambda peer: az_out.at[peer], az_in.at[my_z], az_s, az_r)
    to_protos(lambda peer: tot_z.at[my_z], tot_z.at[my_z], tz_s, tz_r)

    await_bytes(r2z, z_n - 1, r2z_r)
    column_pass(jnp.sum(r2z[...].astype(F32), axis=0))

    own_rows = pl.ds(pl.multiple_of(my_y * LANES, LANES), LANES)
    for k in range(COLS // CHUNK):
        cols = slice(k * CHUNK, (k + 1) * CHUNK)
        scaled = t[own_rows, cols] * v[0:1, cols]
        e[0:LANES, cols] = scaled.astype(BF16)
        halves = scaled[:, :LANES] + scaled[:, LANES:]
        part[0:LANES, :] = halves if k == 0 else part[0:LANES, :] + halves
    r3p[my_c] = lane_sums(part, 1)
    to_crops(lambda peer: r3p.at[my_c], r3p.at[my_c], r3p_s, r3p_r)
    sums = lax.dot_general(e[0:LANES, :], ws[...], NT, preferred_element_type=F32)
    for c in range(c_n):
        for g in range(2):
            ct_out[c, g] = sums[64 * g + 8 * c : 64 * g + 8 * c + 8, :].astype(BF16)
    to_crops(lambda peer: ct_out.at[peer], ct_in.at[my_c], ct_s, ct_r)
    ct_in[my_c] = ct_out[my_c]

    await_bytes(az_in, z_n - 1, az_r)
    az_in[my_z] = az_out[my_z]
    a_all[my_z] = jnp.sum(az_in[...].astype(F32), axis=0)
    to_protos(lambda peer: a_all.at[my_z], a_all.at[my_z], ag_s, ag_r)

    await_bytes(r3p, c_n - 1, r3p_r)
    r3z[my_z] = jnp.sum(r3p[...], axis=0)
    to_protos(lambda peer: r3z.at[my_z], r3z.at[my_z], r3z_s, r3z_r)
    await_bytes(ct_in, c_n - 1, ct_r)
    total = jnp.sum(ct_in[...].astype(F32), axis=0)
    for g in range(2):
        for k in range(4):
            cz_out[4 * g + k] = total[g, :, k * LANES : (k + 1) * LANES].astype(BF16)
    to_protos(lambda peer: cz_out.at[lax.rem(peer, 8)], cz_in.at[my_z], cz_s, cz_r)
    cz_in[my_z] = cz_out[lax.rem(my_z, 8)]

    images = ROWS // c_n
    lane = lax.broadcasted_iota(jnp.int32, (images, LANES), 1)
    row = lax.broadcasted_iota(jnp.int32, (images, LANES), 0)

    def as_column(values, first, rows):
        n = values.shape[1]
        wide = jnp.broadcast_to(values, (rows, n))
        picked = jnp.where(lane[:rows, :n] == row[:rows, :n] + first, wide, jnp.zeros_like(wide))
        return jnp.sum(picked, axis=1, keepdims=True)

    loads[5].wait()
    weights = as_column(weight[...].astype(F32), 0, images)
    x = sf[...].astype(F32)
    unit = su[my_c].astype(F32)
    norm = lax.rsqrt(jnp.sum(x * x, axis=1, keepdims=True) + EPSILON)
    await_bytes(pairs, c_n - 1, pr_r)
    views = [as_column(pairs[c], my_c * 8, 8) > 0.5 for c in range(c_n)]
    await_bytes(tot_z, z_n - 1, tz_r)
    totals = as_column(jnp.sum(tot_z[...], axis=0), side * images, images)
    await_bytes(r3z, z_n - 1, r3z_r)
    last = 1.0 / jnp.sum(r3z[...], axis=0)
    scales = [as_column(last, images * g + my_c * 8, 8) for g in range(2)]

    await_bytes(cz_in, z_n - 1, cz_r)
    mine = lax.rem(my_z, 8)
    c_tiles[mine] = jnp.sum(cz_in[...].astype(F32), axis=0)

    def near(k):
        offset = k + z_n - 4 + jnp.where(k >= 4, 1, 0)
        peer = lax.rem(my_z + offset, z_n)
        push(c_tiles.at[mine], c_tiles.at[mine], cg_s, cg_r, "proto", peer)

    every(7, near)
    await_bytes(a_all, z_n - 1, ag_r)
    for g in range(8):
        for h in range(2):
            grad_ref[g * 8 : g * 8 + 8, h * 256 : (h + 1) * 256] = a_all[2 * g + h] / totals[g * 8 : g * 8 + 8]

    await_bytes(c_tiles, 7, cg_r)
    sides = [
        jnp.concatenate([c_tiles[4 * g + k] for k in range(4)], axis=1) * scales[g] for g in range(2)
    ]
    for c in range(c_n):
        pick_out[c] = jnp.where(views[c], sides[1], sides[0])
    to_crops(lambda peer: pick_out.at[peer], pick_in.at[my_c], ca_s, ca_r)
    pick_in[my_c] = pick_out[my_c]
    await_bytes(pick_in, c_n - 1, ca_r)

    chosen = pick_in[...].reshape(images, ROWS)
    back = (weights * 10.0) * (grad_ref[...] - chosen)
    cross = jnp.sum(unit * chosen, axis=1, keepdims=True) * 10.0
    along = jnp.sum(x * back, axis=1, keepdims=True)
    grad_ref[...] = norm * back - norm * norm * norm * x * along
    losses = jnp.broadcast_to(jnp.log(totals) - cross, (images, images))
    eye = lane[:, :images] == row[:, :images]
    loss_ref[...] = jnp.sum(jnp.where(eye, losses, 0.0), axis=0, keepdims=True)

    for ref, n, sem in (
        (su, y_n - 1, tu_s), (su, y_n - 1, th_s),
        (su, c_n // 2 - 1, su_s), (su, c_n // 2, sh_s), (pairs, c_n - 1, pr_s),
        (r1p, c_n - 1, r1p_s), (r1z, z_n - 1, r1z_s),
        (r2p, c_n - 1, r2p_s), (r2z, z_n - 1, r2z_s), (tot_p, c_n - 1, tp_s),
        (tot_z, z_n - 1, tz_s), (a_in, c_n - 1, a_s),
        (az_in, z_n - 1, az_s), (a_all, z_n - 1, ag_s), (ct_in, c_n - 1, ct_s),
        (cz_in, z_n - 1, cz_s), (c_tiles, 7, cg_s), (pick_in, c_n - 1, ca_s),
        (r3p, c_n - 1, r3p_s), (r3z, z_n - 1, r3z_s),
    ):
        await_bytes(ref, n, sem)


def solution(mesh):
    y_n, c_n, z_n = (mesh.shape[a] for a in ("image", "crop", "proto"))

    def step(teacher_feats, student_feats, teacher_protos, student_protos, pairing, row_weight):
        images, views, width = teacher_feats.shape
        vmem = pl.BlockSpec(memory_space=pltpu.VMEM)
        hbm = pl.BlockSpec(memory_space=pl.ANY)
        dma = pltpu.SemaphoreType.DMA
        ram = pltpu.VMEM
        grad, loss = pl.pallas_call(
            functools.partial(kernel, y_n, c_n, z_n),
            out_shape=(
                jax.ShapeDtypeStruct((images, width), F32),
                jax.ShapeDtypeStruct((1, images), F32),
            ),
            in_specs=[hbm] * 6,
            out_specs=(vmem, vmem),
            scratch_shapes=[
                ram((images, views, width), BF16),
                ram((images, width), BF16),
                ram((1, images), jnp.int32),
                ram((1, images), BF16),
                ram((width, COLS), BF16),
                ram((width, COLS), BF16),
                ram((width, COLS), BF16),
                ram((width, COLS), BF16),
                ram((ROWS, COLS), F32),
                ram((ROWS, COLS), BF16),
                ram((y_n, views, images, width), BF16),
                ram((c_n, images, width), BF16),
                ram((ROWS, LANES), F32),
                ram((ROWS, LANES), F32),
                ram((ROWS, LANES), F32),
                ram((8, COLS), F32),
                ram((8, COLS), F32),
                ram((c_n, 4, LANES), F32),
                ram((z_n, 4, LANES), BF16),
                ram((c_n, 4, LANES), F32),
                ram((z_n, 4, LANES), BF16),
                ram((c_n, 4, LANES), F32),
                ram((4, 1, LANES), F32),
                ram((z_n, 1, LANES), F32),
                ram((c_n, 1, images), F32),
                ram((c_n, images, width), BF16),
                ram((c_n, images, width), BF16),
                ram((z_n, 8, 256), BF16),
                ram((z_n, 8, 256), BF16),
                ram((z_n, 8, 256), F32),
                ram((c_n, 2, 8, width), BF16),
                ram((c_n, 2, 8, width), BF16),
                ram((8, 8, LANES), BF16),
                ram((z_n, 8, LANES), BF16),
                ram((8, 8, LANES), F32),
                ram((c_n, 8, width), F32),
                ram((c_n, 8, width), F32),
                ram((c_n, 1, LANES), F32),
                ram((z_n, 1, LANES), F32),
                dma((6,)),
                dma((y_n,)),
                dma((y_n,)),
            ]
            + [dma(())] * 38,
            compiler_params=pltpu.CompilerParams(collective_id=0, has_side_effects=True),
        )(
            teacher_feats,
            student_feats.reshape(images, width),
            pairing,
            row_weight,
            teacher_protos,
            student_protos,
        )
        return grad.reshape(1, images, width), loss

    return jax.shard_map(
        step,
        mesh=mesh,
        in_specs=(
            P("image", None, None),
            P("crop", "image", None),
            P(None, ("crop", "proto")),
            P(None, ("crop", "proto")),
            P("crop", "image"),
            P("crop", "image"),
        ),
        out_specs=(P("crop", "image", None), P("crop", "image")),
        check_vma=False,
    )
```

time: 82.3 us -> 75.7 us (0.920)
  Pallas kernels: 77.2 us -> 72.2 us
  local copies, waits for them, and re-layouts: 4.32 us -> 2.74 us
    pallas_call x1, Pallas kernels: 77.2 us -> 72.2 us  [step(): pl.pallas_call(functools.partial(kernel, y_n, c_n, z_n), out_shape=(jax.S...]
    transpose x1 -> x0, local copies, waits for them, and re-layouts: 1.57 us -> none  [step(): jnp.transpose(teacher_feats, (1, 0, 2)).reshape(views * images, width)]
where the time goes in v2:
time: 75.7 us; the launch traced here: 75.6 us
  Pallas kernels  72.2 us (95%)
  local copies, waits for them, and re-layouts  2.74 us (4%)
    pallas_call x1, Pallas kernels, step(): pl.pallas_call(functools.partial(kernel, y_n, c_n, z_n), out_shape=(jax.S...  72.2 us
    unnamed x2, local copies, waits for them, and re-layouts  2.74 us

profile of v2, /device:TPU:1, one launch (start us, length us, event | category | flops | bytes accessed | tf_op | source)
XLA Modules:
  0.0 75.6 jit_solution(15619172374156745325)
XLA Ops:
  0.6 72.2 %shard_map.77 = (f32[64,512]{1,0:T(8,128)}, f32[1,64]{1,0:T(1,128)}) custom-call(bf16[64,2,512]{2,1,0:T(2,128)(2,1)} %tf_hbm.1, bf16[64,512]{1,0:T(8,128)(2,1)} %bitcast.3, s32[1,64]{1,0:T(1,128)} %pair_hbm.1, bf16[1,64]{1,0:T(2,128)(2,1)} %weight_hbm.1, bf16[512,2048]{1,0:T(8,128)(2,1)} %tp_hbm.1, bf16[512,2048]{1,0:T(8,128)(2,1)} %sp_hbm.1), custom_call_target="tpu_custom_call" | custom-call | tf_op jit(solution)/shard_map/pallas_call | solution.py:382
  72.8 1.6 %copy.10 = f32[1,64,512]{2,1,0:T(8,128)} copy(f32[1,64,512]{2,1,0:T(8,128)} %bitcast.2) | data formatting | bytes 262144
  74.4 1.2 %copy.11 = f32[1,64]{1,0:T(1,128)} copy(f32[1,64]{1,0:T(1,128)} %get-tuple-element.9) | data formatting | bytes 512

commit v3 on v2

--- a/solution.py
+++ b/solution.py
@@ -8,6 +8,9 @@
 from jax.sharding import PartitionSpec as P
 
 EPSILON = 1e-06
+LOG2_E = 1.4426950408889634
+TEACHER = 25.0 * LOG2_E
+STUDENT = 10.0 * LOG2_E
 MESH = pl.DeviceIdType.MESH
 F32 = jnp.float32
 BF16 = jnp.bfloat16
@@ -26,14 +29,18 @@
     return x * lax.rsqrt(jnp.sum(x * x, axis=1, keepdims=True) + EPSILON)
 
 
-def unit_columns(raw, out):
-    def chunk(j):
+def column_scales(raw, out):
+    def chunk(j, carry):
         cols = pl.ds(pl.multiple_of(j * LANES, LANES), LANES)
-        w = raw[:, cols].astype(F32)
-        scale = lax.rsqrt(jnp.sum(w * w, axis=0, keepdims=True) + EPSILON)
-        out[:, cols] = (w * scale).astype(BF16)
-
-    every(COLS // LANES, chunk)
+        sums = jnp.zeros((8, LANES), F32)
+        for r in range(8):
+            w = raw[64 * r : 64 * r + 64, cols].astype(F32)
+            sums = sums + jnp.sum((w * w).reshape(8, 8, LANES), axis=0)
+        scale = lax.rsqrt(jnp.sum(sums, axis=0, keepdims=True) + EPSILON)
+        out[:, cols] = jnp.broadcast_to(scale, (8, LANES))
+        return carry
+
+    lax.fori_loop(0, COLS // LANES, chunk, 0, unroll=4)
 
 
 def lane_sums(ref, groups):
@@ -47,7 +54,7 @@
     y_n, c_n, z_n,
     tf_hbm, sf_hbm, pair_hbm, weight_hbm, tp_hbm, sp_hbm,
     grad_ref, loss_ref,
-    tf, sf, pair, weight, tp, sp, wt, ws, t, e, tu, su, part, spart, ubuf, v, csum,
+    tf, sf, pair, weight, tp, sp, t_scale, s_scale, t, e, tu, su, part, spart, ubuf, v, csum,
     r1p, r1z, r2p, r2z, tot_p, tot_sum, tot_z, pairs,
     a_out, a_in, az_out, az_in, a_all,
     ct_out, ct_in, cz_out, cz_in, c_tiles, pick_out, pick_in, r3p, r3z,
@@ -119,7 +126,7 @@
     loads[4].wait()
     pairs[my_c] = pair[...].astype(F32)
     loads[2].wait()
-    unit_columns(tp, wt)
+    column_scales(tp, t_scale)
 
     pl.semaphore_wait(barrier, y_n + c_n + z_n - 3)
 
@@ -138,15 +145,17 @@
     to_crops(lambda peer: pairs.at[my_c], pairs.at[my_c], pr_s, pr_r)
 
     def transport(y, first):
-        def chunk(j):
-            cols = pl.ds(pl.multiple_of(j * CHUNK, CHUNK), CHUNK)
-            rows = tu[y].reshape(LANES, ROWS)
-            terms = jnp.exp(jnp.dot(rows, wt[:, cols], preferred_element_type=F32) * 25.0)
-            t[pl.ds(pl.multiple_of(y * LANES, LANES), LANES), cols] = terms
-            sums = jnp.sum(terms.reshape(LANES // 8, 8, CHUNK), axis=0)
-            csum[:, cols] = sums if first else csum[:, cols] + sums
-
-        every(COLS // CHUNK, chunk)
+        def chunk(i):
+            for k in range(4):
+                cols = pl.ds(pl.multiple_of((i * 4 + k) * CHUNK, CHUNK), CHUNK)
+                rows = tu[y].reshape(LANES, ROWS)
+                product = jnp.dot(rows, tp[:, cols], preferred_element_type=F32)
+                terms = jnp.exp2(product * (t_scale[0:1, cols] * TEACHER))
+                t[pl.ds(pl.multiple_of(y * LANES, LANES), LANES), cols] = terms
+                sums = jnp.sum(terms.reshape(LANES // 8, 8, CHUNK), axis=0)
+                csum[:, cols] = sums if first else csum[:, cols] + sums
+
+        every(2, chunk)
 
     def hand_over(y):
         pltpu.make_async_copy(tu.at[y, side], tu.at[y, side], tu_r.at[y]).wait()
@@ -158,12 +167,19 @@
     others = [lax.rem(my_y + k, y_n) for k in (1, 3, 2)]
     transport(my_y, True)
     loads[3].wait()
-    unit_columns(sp, ws)
+    column_scales(sp, s_scale)
     hand_over(others[0])
     hand_over(others[1])
     handed(others[0])
     transport(others[0], False)
     hand_over(others[2])
+    await_bytes(su, c_n // 2 - 1, su_r)
+
+    def hand_students(k):
+        slot = lax.rem(my_c + 2 * k + 2, c_n)
+        push(su.at[slot], su.at[slot], sh_s, sh_r, "crop", partner)
+
+    every(c_n // 2 - 1, hand_students)
     handed(others[1])
     transport(others[1], False)
     handed(others[2])
@@ -208,24 +224,22 @@
     r1p[my_c] = row_pass()
     to_crops(lambda peer: r1p.at[my_c], r1p.at[my_c], r1p_s, r1p_r)
 
-    await_bytes(su, c_n // 2 - 1, su_r)
-
-    def hand_students(k):
-        slot = lax.rem(my_c + 2 * k + 2, c_n)
-        push(su.at[slot], su.at[slot], sh_s, sh_r, "crop", partner)
-
-    every(c_n // 2 - 1, hand_students)
     await_bytes(su, c_n // 2, sh_r)
     spart[...] = jnp.zeros_like(spart)
 
-    def student(j):
-        cols = pl.ds(pl.multiple_of(j * CHUNK, CHUNK), CHUNK)
-        rows = su[...].reshape(ROWS, ROWS)
-        terms = jnp.exp(jnp.dot(rows, ws[:, cols], preferred_element_type=F32) * 10.0)
-        spart[...] += terms[:, :LANES] + terms[:, LANES:]
-        e[:, cols] = terms.astype(BF16)
-
-    every(COLS // CHUNK, student)
+    def student(i):
+        for k in range(2):
+            cols = pl.ds(pl.multiple_of((2 * i + k) * CHUNK, CHUNK), CHUNK)
+            for h in range(2):
+                some = slice(256 * h, 256 * h + 256)
+                rows = su[4 * h : 4 * h + 4].reshape(256, ROWS)
+                product = jnp.dot(rows, sp[:, cols], preferred_element_type=F32)
+                scale = s_scale[0:1, cols]
+                terms = jnp.exp2(product * (scale * STUDENT))
+                spart[some, :] += terms[:, :LANES] + terms[:, LANES:]
+                e[some, cols] = (terms * scale).astype(BF16)
+
+    every(COLS // CHUNK // 2, student)
 
     await_bytes(r1p, c_n - 1, r1p_r)
     r1z[my_z] = jnp.sum(r1p[...], axis=0).astype(BF16)
@@ -233,7 +247,7 @@
 
     for j in range(2):
         some = slice(j * CHUNK, (j + 1) * CHUNK)
-        back = lax.dot_general(e[...], ws[some, :], NT, preferred_element_type=F32)
+        back = lax.dot_general(e[...], sp[some, :], NT, preferred_element_type=F32)
         a_out[:, :, some] = back.astype(BF16).reshape(c_n, ROWS // c_n, CHUNK)
     to_crops(lambda peer: a_out.at[peer], a_in.at[my_c], a_s, a_r)
     tot_p[my_c] = lane_sums(spart, 4)
@@ -244,6 +258,9 @@
     r2p[my_c] = row_pass()
     to_crops(lambda peer: r2p.at[my_c], r2p.at[my_c], r2p_s, r2p_r)
 
+    await_bytes(r2p, c_n - 1, r2p_r)
+    r2z[my_z] = jnp.sum(r2p[...], axis=0).astype(BF16)
+    to_protos(lambda peer: r2z.at[my_z], r2z.at[my_z], r2z_s, r2z_r)
     await_bytes(a_in, c_n - 1, a_r)
     a_in[my_c] = a_out[my_c]
     for g in range(8):
@@ -259,9 +276,6 @@
         tot_sum[q] = whole[q : q + 1, :]
     tot_z[my_z] = tot_sum[my_c // 2]
 
-    await_bytes(r2p, c_n - 1, r2p_r)
-    r2z[my_z] = jnp.sum(r2p[...], axis=0).astype(BF16)
-    to_protos(lambda peer: r2z.at[my_z], r2z.at[my_z], r2z_s, r2z_r)
     to_protos(lambda peer: az_out.at[peer], az_in.at[my_z], az_s, az_r)
     to_protos(lambda peer: tot_z.at[my_z], tot_z.at[my_z], tz_s, tz_r)
 
@@ -272,12 +286,12 @@
     for k in range(COLS // CHUNK):
         cols = slice(k * CHUNK, (k + 1) * CHUNK)
         scaled = t[own_rows, cols] * v[0:1, cols]
-        e[0:LANES, cols] = scaled.astype(BF16)
+        e[0:LANES, cols] = (scaled * s_scale[0:1, cols]).astype(BF16)
         halves = scaled[:, :LANES] + scaled[:, LANES:]
         part[0:LANES, :] = halves if k == 0 else part[0:LANES, :] + halves
     r3p[my_c] = lane_sums(part, 1)
     to_crops(lambda peer: r3p.at[my_c], r3p.at[my_c], r3p_s, r3p_r)
-    sums = lax.dot_general(e[0:LANES, :], ws[...], NT, preferred_element_type=F32)
+    sums = lax.dot_general(e[0:LANES, :], sp[...], NT, preferred_element_type=F32)
     for c in range(c_n):
         for g in range(2):
             ct_out[c, g] = sums[64 * g + 8 * c : 64 * g + 8 * c + 8, :].astype(BF16)
@@ -370,13 +384,18 @@
         await_bytes(ref, n, sem)
 
 
+def deliver(grad_in, loss_in, grad_ref, loss_ref):
+    grad_ref[0] = grad_in[...]
+    loss_ref[...] = loss_in[...]
+
+
 def solution(mesh):
     y_n, c_n, z_n = (mesh.shape[a] for a in ("image", "crop", "proto"))
 
     def step(teacher_feats, student_feats, teacher_protos, student_protos, pairing, row_weight):
         images, views, width = teacher_feats.shape
         vmem = pl.BlockSpec(memory_space=pltpu.VMEM)
-        hbm = pl.BlockSpec(memory_space=pl.ANY)
+        hbm = pl.BlockSpec(memory_space=pltpu.HBM)
         dma = pltpu.SemaphoreType.DMA
         ram = pltpu.VMEM
         grad, loss = pl.pallas_call(
@@ -394,8 +413,8 @@
                 ram((1, images), BF16),
                 ram((width, COLS), BF16),
                 ram((width, COLS), BF16),
-                ram((width, COLS), BF16),
-                ram((width, COLS), BF16),
+                ram((8, COLS), F32),
+                ram((8, COLS), F32),
                 ram((ROWS, COLS), F32),
                 ram((ROWS, COLS), BF16),
                 ram((y_n, views, images, width), BF16),
@@ -432,16 +451,32 @@
                 dma((y_n,)),
             ]
             + [dma(())] * 38,
-            compiler_params=pltpu.CompilerParams(collective_id=0, has_side_effects=True),
+            compiler_params=pltpu.CompilerParams(
+                collective_id=0, has_side_effects=True, vmem_limit_bytes=32 * 1024 * 1024
+            ),
         )(
-            teacher_feats,
-            student_feats.reshape(images, width),
-            pairing,
-            row_weight,
-            teacher_protos,
-            student_protos,
+            *(
+                pltpu.with_memory_space_constraint(x, pltpu.HBM)
+                for x in (
+                    teacher_feats,
+                    student_feats.reshape(images, width),
+                    pairing,
+                    row_weight,
+                    teacher_protos,
+                    student_protos,
+                )
+            )
         )
-        return grad.reshape(1, images, width), loss
+        return pl.pallas_call(
+            deliver,
+            out_shape=(
+                jax.ShapeDtypeStruct((1, images, width), F32),
+                jax.ShapeDtypeStruct((1, images), F32),
+            ),
+            in_specs=[vmem] * 2,
+            out_specs=(vmem, vmem),
+            compiler_params=pltpu.CompilerParams(vmem_limit_bytes=2 * 1024 * 1024),
+        )(grad, loss)
 
     return jax.shard_map(
         step,

time: 75.7 us -> 70.3 us (0.929)
  local copies, waits for them, and re-layouts: 2.74 us -> 0 us
  Pallas kernels: 72.2 us -> 69.5 us
    pallas_call x1, Pallas kernels: 72.2 us -> 68.9 us  [step(): pl.pallas_call(functools.partial(kernel, y_n, c_n, z_n), out_shape=(jax.S...]
    unnamed x2 -> x0, local copies, waits for them, and re-layouts: 2.74 us -> none
where the time goes in v3:
time: 70.3 us; the launch traced here: 70.2 us
  Pallas kernels  69.5 us (99%)
    pallas_call x1, Pallas kernels, step(): pl.pallas_call(functools.partial(kernel, y_n, c_n, z_n), out_shape=(jax.S...  68.9 us

profile of v3, /device:TPU:1, one launch (start us, length us, event | category | flops | bytes accessed | tf_op | source)
XLA Modules:
  0.0 70.2 jit_solution(9244479564137561356)
XLA Ops:
  0.6 68.9 %shard_map.77 = (f32[64,512]{1,0:T(8,128)S(1)}, f32[1,64]{1,0:T(1,128)S(1)}) custom-call(bf16[64,2,512]{2,1,0:T(2,128)(2,1)} %tf_hbm.1, bf16[64,512]{1,0:T(8,128)(2,1)} %bitcast.1, s32[1,64]{1,0:T(1,128)} %pair_hbm.1, bf16[1,64]{1,0:T(2,128)(2,1)} %weight_hbm.1, bf16[512,2048]{1,0:T(8,128)(2,1)} %tp_hbm.1, bf16[512,2048]{1,0:T(8,128)(2,1)} %sp_hbm.1), custom_call_target="tpu_custom_call" | custom-call | tf_op jit(solution)/shard_map/pallas_call | solution.py:401
  69.5 0.7 shard_map.78

commit v4 on v3

--- a/solution.py
+++ b/solution.py
@@ -56,12 +56,12 @@
     grad_ref, loss_ref,
     tf, sf, pair, weight, tp, sp, t_scale, s_scale, t, e, tu, su, part, spart, ubuf, v, csum,
     r1p, r1z, r2p, r2z, tot_p, tot_sum, tot_z, pairs,
-    a_out, a_in, az_out, az_in, a_all,
+    a_out, a_mid, a_pre, a_in, az_out, az_in, a_all, col_sums,
     ct_out, ct_in, cz_out, cz_in, c_tiles, pick_out, pick_in, r3p, r3z,
     load, tu_r, th_r,
     tu_s, th_s, su_s, su_r, sh_s, sh_r, pr_s, pr_r, r1p_s, r1p_r, r1z_s, r1z_r,
     r2p_s, r2p_r, r2z_s, r2z_r, tp_s, tp_r, tz_s, tz_r, a_s, a_r, az_s, az_r, ag_s, ag_r,
-    ct_s, ct_r, cz_s, cz_r, cg_s, cg_r, ca_s, ca_r, r3p_s, r3p_r, r3z_s, r3z_r,
+    am_s, am_r, cs_s, cs_r, ct_s, ct_r, cz_s, cz_r, cg_s, cg_r, ca_s, ca_r, r3p_s, r3p_r, r3z_s, r3z_r,
 ):
     my_y, my_c, my_z = (lax.axis_index(a) for a in ("image", "crop", "proto"))
     side = lax.rem(my_c, 2)
@@ -73,8 +73,6 @@
             ((tf_hbm, tf), (sf_hbm, sf), (tp_hbm, tp), (sp_hbm, sp), (pair_hbm, pair), (weight_hbm, weight))
         )
     ]
-    for copy in loads:
-        copy.start()
 
     def far_first(k):
         step = k + 1
@@ -106,17 +104,19 @@
 
     barrier = pltpu.get_barrier_semaphore()
 
-    def greet(axis, me, n):
-        def one(k):
-            pl.semaphore_signal(
-                barrier, inc=1, device_id={axis: lax.rem(me + k + 1, n)}, device_id_type=MESH
-            )
-
-        every(n - 1, one)
-
-    greet("proto", my_z, z_n)
-    greet("image", my_y, y_n)
-    greet("crop", my_c, c_n)
+    def greet(peer):
+        pl.semaphore_signal(barrier, inc=1, device_id=peer, device_id_type=MESH)
+
+    def plane_peer(k):
+        return {
+            "image": lax.rem(my_y + (k + 1) // c_n, y_n),
+            "crop": lax.rem(my_c + lax.rem(k + 1, c_n), c_n),
+        }
+
+    every(z_n - 1, lambda k: greet({"proto": lax.rem(my_z + far_first(k), z_n)}))
+    for copy in loads:
+        copy.start()
+    every(y_n * c_n - 1, lambda k: greet(plane_peer(k)))
 
     loads[0].wait()
     for g in range(2):
@@ -128,23 +128,7 @@
     loads[2].wait()
     column_scales(tp, t_scale)
 
-    pl.semaphore_wait(barrier, y_n + c_n + z_n - 3)
-
-    def give_rows(k):
-        peer = lax.rem(my_y + 2 * k + 1 - 3 * (k // 2), y_n)
-        push(tu.at[my_y, side], tu.at[my_y, side], tu_s, tu_r.at[my_y], "image", peer)
-
-    every(y_n - 1, give_rows)
-
-    def give_students(k):
-        peer = lax.rem(my_c + 2 * k + 2, c_n)
-        push(su.at[my_c], su.at[my_c], su_s, su_r, "crop", peer)
-
-    every(c_n // 2 - 1, give_students)
-    push(su.at[my_c], su.at[my_c], sh_s, sh_r, "crop", partner)
-    to_crops(lambda peer: pairs.at[my_c], pairs.at[my_c], pr_s, pr_r)
-
-    def transport(y, first):
+    def transport(y, own):
         def chunk(i):
             for k in range(4):
                 cols = pl.ds(pl.multiple_of((i * 4 + k) * CHUNK, CHUNK), CHUNK)
@@ -152,10 +136,39 @@
                 product = jnp.dot(rows, tp[:, cols], preferred_element_type=F32)
                 terms = jnp.exp2(product * (t_scale[0:1, cols] * TEACHER))
                 t[pl.ds(pl.multiple_of(y * LANES, LANES), LANES), cols] = terms
-                sums = jnp.sum(terms.reshape(LANES // 8, 8, CHUNK), axis=0)
-                csum[:, cols] = sums if first else csum[:, cols] + sums
+                if own:
+                    csum[:, cols] = jnp.sum(terms.reshape(LANES // 8, 8, CHUNK), axis=0)
 
         every(2, chunk)
+
+    transport(my_y, True)
+    for k in range(COLS // LANES):
+        cols = slice(k * LANES, (k + 1) * LANES)
+        col_sums[my_y, :, cols] = jnp.sum(csum[:, cols], axis=0, keepdims=True)
+    loads[3].wait()
+    column_scales(sp, s_scale)
+
+    pl.semaphore_wait(barrier, y_n * c_n + z_n - 2)
+
+    def give_sums(k):
+        peer = lax.rem(my_y + 2 * k + 1 - 3 * (k // 2), y_n)
+        push(col_sums.at[my_y], col_sums.at[my_y], cs_s, cs_r, "image", peer)
+
+    every(y_n - 1, give_sums)
+
+    def give_rows(k):
+        peer = lax.rem(my_y + 2 * k + 1 - 3 * (k // 2), y_n)
+        push(tu.at[my_y, side], tu.at[my_y, side], tu_s, tu_r.at[my_y], "image", peer)
+
+    every(y_n - 1, give_rows)
+
+    def give_students(k):
+        peer = lax.rem(my_c + 2 * k + 2, c_n)
+        push(su.at[my_c], su.at[my_c], su_s, su_r, "crop", peer)
+
+    every(c_n // 2 - 1, give_students)
+    push(su.at[my_c], su.at[my_c], sh_s, sh_r, "crop", partner)
+    to_crops(lambda peer: pairs.at[my_c], pairs.at[my_c], pr_s, pr_r)
 
     def hand_over(y):
         pltpu.make_async_copy(tu.at[y, side], tu.at[y, side], tu_r.at[y]).wait()
@@ -164,10 +177,54 @@
     def handed(y):
         pltpu.make_async_copy(tu.at[y, side], tu.at[y, side], th_r.at[y]).wait()
 
+    def set_v(sums):
+        for k, s in enumerate(sums):
+            v[:, k * LANES : (k + 1) * LANES] = jnp.broadcast_to(
+                1.0 / jnp.sum(s, axis=0, keepdims=True), (8, LANES)
+            )
+
+    def row_pass(first, n):
+        def block(r, carry):
+            rows = pl.ds(pl.multiple_of(first + r * 8, 8), 8)
+            total = t[rows, 0:LANES] * v[:, 0:LANES]
+            for k in range(1, COLS // LANES):
+                cols = slice(k * LANES, (k + 1) * LANES)
+                total = total + t[rows, cols] * v[:, cols]
+            part[pl.ds(pl.multiple_of(r * 8, 8), 8), :] = total
+            return carry
+
+        lax.fori_loop(0, n // 8, block, 0, unroll=4)
+        return lane_sums(part, n // LANES)
+
+    def column_pass(row_sums):
+        u = 1.0 / row_sums
+        for q in range(ROWS // LANES):
+            ubuf[q * LANES : (q + 1) * LANES, :] = jnp.broadcast_to(u[q : q + 1, :], (LANES, LANES)).T
+
+        def block(r, sums):
+            rows = pl.ds(pl.multiple_of(r * 8, 8), 8)
+            scale = ubuf[rows, :]
+            return tuple(
+                s + t[rows, k * LANES : (k + 1) * LANES] * scale for k, s in enumerate(sums)
+            )
+
+        zero = tuple(jnp.zeros((8, LANES), F32) for _ in range(COLS // LANES))
+        set_v(lax.fori_loop(0, ROWS // 8, block, zero, unroll=4))
+
+    await_bytes(col_sums, y_n - 1, cs_r)
+    v[...] = jnp.broadcast_to(1.0 / jnp.sum(col_sums[...], axis=0), (8, COLS))
+    mine_1 = my_y * c_n + my_c
+    r1p[mine_1] = row_pass(my_y * LANES, LANES)
+
+    def give_first(k):
+        pltpu.make_async_remote_copy(
+            src_ref=r1p.at[mine_1], dst_ref=r1p.at[mine_1], send_sem=r1p_s, recv_sem=r1p_r,
+            device_id=plane_peer(k), device_id_type=MESH,
+        ).start()
+
+    every(y_n * c_n - 1, give_first)
+
     others = [lax.rem(my_y + k, y_n) for k in (1, 3, 2)]
-    transport(my_y, True)
-    loads[3].wait()
-    column_scales(sp, s_scale)
     hand_over(others[0])
     hand_over(others[1])
     handed(others[0])
@@ -185,44 +242,10 @@
     handed(others[2])
     transport(others[2], False)
 
-    def set_v(sums):
-        for k, s in enumerate(sums):
-            v[:, k * LANES : (k + 1) * LANES] = jnp.broadcast_to(
-                1.0 / jnp.sum(s, axis=0, keepdims=True), (8, LANES)
-            )
-
-    set_v([csum[:, k * LANES : (k + 1) * LANES] for k in range(COLS // LANES)])
-
-    def row_pass():
-        def block(r, carry):
-            rows = pl.ds(pl.multiple_of(r * 8, 8), 8)
-            total = t[rows, 0:LANES] * v[:, 0:LANES]
-            for k in range(1, COLS // LANES):
-                cols = slice(k * LANES, (k + 1) * LANES)
-                total = total + t[rows, cols] * v[:, cols]
-            part[rows, :] = total
-            return carry
-
-        lax.fori_loop(0, ROWS // 8, block, 0, unroll=4)
-        return lane_sums(part, 4)
-
-    def column_pass(row_sums):
-        u = 1.0 / row_sums
-        for q in range(ROWS // LANES):
-            ubuf[q * LANES : (q + 1) * LANES, :] = jnp.broadcast_to(u[q : q + 1, :], (LANES, LANES)).T
-
-        def block(r, sums):
-            rows = pl.ds(pl.multiple_of(r * 8, 8), 8)
-            scale = ubuf[rows, :]
-            return tuple(
-                s + t[rows, k * LANES : (k + 1) * LANES] * scale for k, s in enumerate(sums)
-            )
-
-        zero = tuple(jnp.zeros((8, LANES), F32) for _ in range(COLS // LANES))
-        set_v(lax.fori_loop(0, ROWS // 8, block, zero, unroll=4))
-
-    r1p[my_c] = row_pass()
-    to_crops(lambda peer: r1p.at[my_c], r1p.at[my_c], r1p_s, r1p_r)
+    await_bytes(r1p, y_n * c_n - 1, r1p_r)
+    firsts = [jnp.sum(r1p[c_n * y : c_n * y + c_n], axis=0) for y in range(y_n)]
+    r1z[my_z] = jnp.concatenate(firsts, axis=0).astype(BF16)
+    to_protos(lambda peer: r1z.at[my_z], r1z.at[my_z], r1z_s, r1z_r)
 
     await_bytes(su, c_n // 2, sh_r)
     spart[...] = jnp.zeros_like(spart)
@@ -241,32 +264,42 @@
 
     every(COLS // CHUNK // 2, student)
 
-    await_bytes(r1p, c_n - 1, r1p_r)
-    r1z[my_z] = jnp.sum(r1p[...], axis=0).astype(BF16)
-    to_protos(lambda peer: r1z.at[my_z], r1z.at[my_z], r1z_s, r1z_r)
-
     for j in range(2):
         some = slice(j * CHUNK, (j + 1) * CHUNK)
         back = lax.dot_general(e[...], sp[some, :], NT, preferred_element_type=F32)
-        a_out[:, :, some] = back.astype(BF16).reshape(c_n, ROWS // c_n, CHUNK)
-    to_crops(lambda peer: a_out.at[peer], a_in.at[my_c], a_s, a_r)
+        for c in range(c_n):
+            a_out[c % 2, c // 2, :, some] = back[64 * c : 64 * c + 64, :].astype(BF16)
+    push(a_out.at[1 - side], a_mid, am_s, am_r, "crop", partner)
     tot_p[my_c] = lane_sums(spart, 4)
     to_crops(lambda peer: tot_p.at[my_c], tot_p.at[my_c], tp_s, tp_r)
+    pltpu.make_async_copy(a_mid, a_mid, am_r).wait()
+    my_x = my_c // 2
+
+    def merge(x):
+        a_pre[x] = (a_out[side, x].astype(F32) + a_mid[x].astype(F32)).astype(BF16)
+
+    every(c_n // 2, merge)
+
+    def give_parts(k):
+        x = lax.rem(my_x + k + 1, c_n // 2)
+        push(a_pre.at[x], a_in.at[my_x], a_s, a_r, "crop", 2 * x + side)
+
+    every(c_n // 2 - 1, give_parts)
 
     await_bytes(r1z, z_n - 1, r1z_r)
     column_pass(jnp.sum(r1z[...].astype(F32), axis=0))
-    r2p[my_c] = row_pass()
+    r2p[my_c] = row_pass(0, ROWS)
     to_crops(lambda peer: r2p.at[my_c], r2p.at[my_c], r2p_s, r2p_r)
 
     await_bytes(r2p, c_n - 1, r2p_r)
     r2z[my_z] = jnp.sum(r2p[...], axis=0).astype(BF16)
     to_protos(lambda peer: r2z.at[my_z], r2z.at[my_z], r2z_s, r2z_r)
-    await_bytes(a_in, c_n - 1, a_r)
-    a_in[my_c] = a_out[my_c]
+    await_bytes(a_in, c_n // 2 - 1, a_r)
+    a_in[my_x] = a_pre[my_x]
     for g in range(8):
         rows = slice(g * 8, g * 8 + 8)
         total = a_in[0, rows, :].astype(F32)
-        for k in range(1, c_n):
+        for k in range(1, c_n // 2):
             total = total + a_in[k, rows, :].astype(F32)
         for h in range(2):
             az_out[2 * g + h] = total[:, h * 256 : (h + 1) * 256].astype(BF16)
@@ -372,16 +405,17 @@
     loss_ref[...] = jnp.sum(jnp.where(eye, losses, 0.0), axis=0, keepdims=True)
 
     for ref, n, sem in (
-        (su, y_n - 1, tu_s), (su, y_n - 1, th_s),
+        (su, y_n - 1, tu_s), (su, y_n - 1, th_s), (col_sums, y_n - 1, cs_s),
         (su, c_n // 2 - 1, su_s), (su, c_n // 2, sh_s), (pairs, c_n - 1, pr_s),
-        (r1p, c_n - 1, r1p_s), (r1z, z_n - 1, r1z_s),
+        (r1p, y_n * c_n - 1, r1p_s), (r1z, z_n - 1, r1z_s),
         (r2p, c_n - 1, r2p_s), (r2z, z_n - 1, r2z_s), (tot_p, c_n - 1, tp_s),
-        (tot_z, z_n - 1, tz_s), (a_in, c_n - 1, a_s),
+        (tot_z, z_n - 1, tz_s), (a_in, c_n // 2 - 1, a_s),
         (az_in, z_n - 1, az_s), (a_all, z_n - 1, ag_s), (ct_in, c_n - 1, ct_s),
         (cz_in, z_n - 1, cz_s), (c_tiles, 7, cg_s), (pick_in, c_n - 1, ca_s),
         (r3p, c_n - 1, r3p_s), (r3z, z_n - 1, r3z_s),
     ):
         await_bytes(ref, n, sem)
+    pltpu.make_async_copy(a_mid, a_mid, am_s).wait()
 
 
 def deliver(grad_in, loss_in, grad_ref, loss_ref):
@@ -424,7 +458,7 @@
                 ram((ROWS, LANES), F32),
                 ram((8, COLS), F32),
                 ram((8, COLS), F32),
-                ram((c_n, 4, LANES), F32),
+                ram((y_n * c_n, 1, LANES), F32),
                 ram((z_n, 4, LANES), BF16),
                 ram((c_n, 4, LANES), F32),
                 ram((z_n, 4, LANES), BF16),
@@ -432,11 +466,14 @@
                 ram((4, 1, LANES), F32),
                 ram((z_n, 1, LANES), F32),
                 ram((c_n, 1, images), F32),
-                ram((c_n, images, width), BF16),
-                ram((c_n, images, width), BF16),
+                ram((2, c_n // 2, images, width), BF16),
+                ram((c_n // 2, images, width), BF16),
+                ram((c_n // 2, images, width), BF16),
+                ram((c_n // 2, images, width), BF16),
                 ram((z_n, 8, 256), BF16),
                 ram((z_n, 8, 256), BF16),
                 ram((z_n, 8, 256), F32),
+                ram((y_n, 1, COLS), F32),
                 ram((c_n, 2, 8, width), BF16),
                 ram((c_n, 2, 8, width), BF16),
                 ram((8, 8, LANES), BF16),
@@ -450,7 +487,7 @@
                 dma((y_n,)),
                 dma((y_n,)),
             ]
-            + [dma(())] * 38,
+            + [dma(())] * 42,
             compiler_params=pltpu.CompilerParams(
                 collective_id=0, has_side_effects=True, vmem_limit_bytes=32 * 1024 * 1024
             ),

time: 70.3 us -> 67.7 us (0.963)
  Pallas kernels: 69.5 us -> 67 us
    pallas_call x1, Pallas kernels: 68.9 us -> 66.3 us  [step(): pl.pallas_call(functools.partial(kernel, y_n, c_n, z_n), out_shape=(jax.S...]
where the time goes in v4:
time: 67.7 us; the launch traced here: 67.6 us
  Pallas kernels  67 us (99%)
    pallas_call x1, Pallas kernels, step(): pl.pallas_call(functools.partial(kernel, y_n, c_n, z_n), out_shape=(jax.S...  66.3 us

profile of v4, /device:TPU:1, one launch (start us, length us, event | category | flops | bytes accessed | tf_op | source)
XLA Modules:
  0.0 67.6 jit_solution(6870431401297449922)
XLA Ops:
  0.6 66.3 %shard_map.77 = (f32[64,512]{1,0:T(8,128)S(1)}, f32[1,64]{1,0:T(1,128)S(1)}) custom-call(bf16[64,2,512]{2,1,0:T(2,128)(2,1)} %tf_hbm.1, bf16[64,512]{1,0:T(8,128)(2,1)} %bitcast.1, s32[1,64]{1,0:T(1,128)} %pair_hbm.1, bf16[1,64]{1,0:T(2,128)(2,1)} %weight_hbm.1, bf16[512,2048]{1,0:T(8,128)(2,1)} %tp_hbm.1, bf16[512,2048]{1,0:T(8,128)(2,1)} %sp_hbm.1), custom_call_target="tpu_custom_call" | custom-call | tf_op jit(solution)/shard_map/pallas_call | solution.py:435
  66.9 0.7 shard_map.78

commit v5 on v4

--- a/solution.py
+++ b/solution.py
@@ -57,11 +57,11 @@
     tf, sf, pair, weight, tp, sp, t_scale, s_scale, t, e, tu, su, part, spart, ubuf, v, csum,
     r1p, r1z, r2p, r2z, tot_p, tot_sum, tot_z, pairs,
     a_out, a_mid, a_pre, a_in, az_out, az_in, a_all, col_sums,
-    ct_out, ct_in, cz_out, cz_in, c_tiles, pick_out, pick_in, r3p, r3z,
+    ct_out, ct_in, cz_out, cz_in, pick_out, pick_in, r3p, r3z,
     load, tu_r, th_r,
     tu_s, th_s, su_s, su_r, sh_s, sh_r, pr_s, pr_r, r1p_s, r1p_r, r1z_s, r1z_r,
     r2p_s, r2p_r, r2z_s, r2z_r, tp_s, tp_r, tz_s, tz_r, a_s, a_r, az_s, az_r, ag_s, ag_r,
-    am_s, am_r, cs_s, cs_r, ct_s, ct_r, cz_s, cz_r, cg_s, cg_r, ca_s, ca_r, r3p_s, r3p_r, r3z_s, r3z_r,
+    am_s, am_r, cs_s, cs_r, ct_s, ct_r, cz_s, cz_r, ca_s, ca_r, r3p_s, r3p_r, r3z_s, r3z_r,
 ):
     my_y, my_c, my_z = (lax.axis_index(a) for a in ("image", "crop", "proto"))
     side = lax.rem(my_c, 2)
@@ -86,7 +86,7 @@
 
     def to_crops(src, dst, sends, recvs):
         def one(k):
-            peer = lax.rem(my_c + k + 1, c_n)
+            peer = lax.rem(my_c + lax.rem(k + 2, c_n - 1) + 1, c_n)
             push(src(peer), dst, sends, recvs, "crop", peer)
 
         every(c_n - 1, one)
@@ -108,9 +108,10 @@
         pl.semaphore_signal(barrier, inc=1, device_id=peer, device_id_type=MESH)
 
     def plane_peer(k):
+        step = lax.rem(k + 15, y_n * c_n - 1) + 1
         return {
-            "image": lax.rem(my_y + (k + 1) // c_n, y_n),
-            "crop": lax.rem(my_c + lax.rem(k + 1, c_n), c_n),
+            "image": lax.rem(my_y + step // c_n, y_n),
+            "crop": lax.rem(my_c + lax.rem(step, c_n), c_n),
         }
 
     every(z_n - 1, lambda k: greet({"proto": lax.rem(my_z + far_first(k), z_n)}))
@@ -151,7 +152,7 @@
     pl.semaphore_wait(barrier, y_n * c_n + z_n - 2)
 
     def give_sums(k):
-        peer = lax.rem(my_y + 2 * k + 1 - 3 * (k // 2), y_n)
+        peer = lax.rem(my_y + 2 - k + 3 * (k // 2), y_n)
         push(col_sums.at[my_y], col_sums.at[my_y], cs_s, cs_r, "image", peer)
 
     every(y_n - 1, give_sums)
@@ -341,11 +342,12 @@
     to_protos(lambda peer: r3z.at[my_z], r3z.at[my_z], r3z_s, r3z_r)
     await_bytes(ct_in, c_n - 1, ct_r)
     total = jnp.sum(ct_in[...].astype(F32), axis=0)
-    for g in range(2):
-        for k in range(4):
-            cz_out[4 * g + k] = total[g, :, k * LANES : (k + 1) * LANES].astype(BF16)
-    to_protos(lambda peer: cz_out.at[lax.rem(peer, 8)], cz_in.at[my_z], cz_s, cz_r)
-    cz_in[my_z] = cz_out[lax.rem(my_z, 8)]
+    mine = lax.rem(my_z, 4)
+    for k in range(4):
+        tile = total[:, :, k * LANES : (k + 1) * LANES].reshape(16, LANES)
+        cz_out[k] = tile.astype(BF16)
+    to_protos(lambda peer: cz_out.at[lax.rem(peer, 4)], cz_in.at[my_z], cz_s, cz_r)
+    cz_in[my_z] = cz_out[mine]
 
     images = ROWS // c_n
     lane = lax.broadcasted_iota(jnp.int32, (images, LANES), 1)
@@ -371,31 +373,33 @@
     scales = [as_column(last, images * g + my_c * 8, 8) for g in range(2)]
 
     await_bytes(cz_in, z_n - 1, cz_r)
-    mine = lax.rem(my_z, 8)
-    c_tiles[mine] = jnp.sum(cz_in[...].astype(F32), axis=0)
-
-    def near(k):
-        offset = k + z_n - 4 + jnp.where(k >= 4, 1, 0)
-        peer = lax.rem(my_z + offset, z_n)
-        push(c_tiles.at[mine], c_tiles.at[mine], cg_s, cg_r, "proto", peer)
-
-    every(7, near)
+    tile = jnp.sum(cz_in[...].astype(F32), axis=0)
+    sides = [tile[8 * g : 8 * g + 8] * scales[g] for g in range(2)]
+    for c in range(c_n):
+        pick_out[c] = jnp.where(views[c], sides[1], sides[0])
+    slot = mine * c_n + my_c
+
+    def give_picks(k):
+        step = lax.rem(k + 15, 4 * c_n - 1) + 1
+        peer_c = lax.rem(my_c + lax.rem(step, c_n), c_n)
+        pltpu.make_async_remote_copy(
+            src_ref=pick_out.at[peer_c], dst_ref=pick_in.at[slot], send_sem=ca_s, recv_sem=ca_r,
+            device_id={"crop": peer_c, "proto": lax.rem(my_z + z_n + 1 - lax.rem(step // c_n + 1, 4), z_n)},
+            device_id_type=MESH,
+        ).start()
+
+    every(4 * c_n - 1, give_picks)
+    pick_in[slot] = pick_out[my_c]
     await_bytes(a_all, z_n - 1, ag_r)
     for g in range(8):
         for h in range(2):
-            grad_ref[g * 8 : g * 8 + 8, h * 256 : (h + 1) * 256] = a_all[2 * g + h] / totals[g * 8 : g * 8 + 8]
-
-    await_bytes(c_tiles, 7, cg_r)
-    sides = [
-        jnp.concatenate([c_tiles[4 * g + k] for k in range(4)], axis=1) * scales[g] for g in range(2)
-    ]
-    for c in range(c_n):
-        pick_out[c] = jnp.where(views[c], sides[1], sides[0])
-    to_crops(lambda peer: pick_out.at[peer], pick_in.at[my_c], ca_s, ca_r)
-    pick_in[my_c] = pick_out[my_c]
-    await_bytes(pick_in, c_n - 1, ca_r)
-
-    chosen = pick_in[...].reshape(images, ROWS)
+            rows = slice(g * 8, g * 8 + 8)
+            grad_ref[rows, h * 256 : (h + 1) * 256] = a_all[2 * g + h] / totals[rows]
+    await_bytes(pick_in, 4 * c_n - 1, ca_r)
+
+    chosen = jnp.concatenate(
+        [jnp.concatenate([pick_in[k * c_n + c] for k in range(4)], axis=1) for c in range(c_n)], axis=0
+    )
     back = (weights * 10.0) * (grad_ref[...] - chosen)
     cross = jnp.sum(unit * chosen, axis=1, keepdims=True) * 10.0
     along = jnp.sum(x * back, axis=1, keepdims=True)
@@ -411,7 +415,7 @@
         (r2p, c_n - 1, r2p_s), (r2z, z_n - 1, r2z_s), (tot_p, c_n - 1, tp_s),
         (tot_z, z_n - 1, tz_s), (a_in, c_n // 2 - 1, a_s),
         (az_in, z_n - 1, az_s), (a_all, z_n - 1, ag_s), (ct_in, c_n - 1, ct_s),
-        (cz_in, z_n - 1, cz_s), (c_tiles, 7, cg_s), (pick_in, c_n - 1, ca_s),
+        (cz_in, z_n - 1, cz_s), (pick_in, 4 * c_n - 1, ca_s),
         (r3p, c_n - 1, r3p_s), (r3z, z_n - 1, r3z_s),
     ):
         await_bytes(ref, n, sem)
@@ -476,18 +480,17 @@
                 ram((y_n, 1, COLS), F32),
                 ram((c_n, 2, 8, width), BF16),
                 ram((c_n, 2, 8, width), BF16),
-                ram((8, 8, LANES), BF16),
-                ram((z_n, 8, LANES), BF16),
-                ram((8, 8, LANES), F32),
-                ram((c_n, 8, width), F32),
-                ram((c_n, 8, width), F32),
+                ram((4, 16, LANES), BF16),
+                ram((z_n, 16, LANES), BF16),
+                ram((c_n, 8, LANES), F32),
+                ram((4 * c_n, 8, LANES), F32),
                 ram((c_n, 1, LANES), F32),
                 ram((z_n, 1, LANES), F32),
                 dma((6,)),
                 dma((y_n,)),
                 dma((y_n,)),
             ]
-            + [dma(())] * 42,
+            + [dma(())] * 40,
             compiler_params=pltpu.CompilerParams(
                 collective_id=0, has_side_effects=True, vmem_limit_bytes=32 * 1024 * 1024
             ),

time: 67.7 us -> 65.9 us (0.973)
  Pallas kernels: 67 us -> 65.1 us
    pallas_call x1, Pallas kernels: 66.3 us -> 64.5 us  [step(): pl.pallas_call(functools.partial(kernel, y_n, c_n, z_n), out_shape=(jax.S...]
where the time goes in v5:
time: 65.9 us; the launch traced here: 65.8 us
  Pallas kernels  65.1 us (99%)
    pallas_call x1, Pallas kernels, step(): pl.pallas_call(functools.partial(kernel, y_n, c_n, z_n), out_shape=(jax.S...  64.5 us

profile of v5, /device:TPU:1, one launch (start us, length us, event | category | flops | bytes accessed | tf_op | source)
XLA Modules:
  0.0 65.8 jit_solution(16108908918797952776)
XLA Ops:
  0.6 64.5 %shard_map.77 = (f32[64,512]{1,0:T(8,128)S(1)}, f32[1,64]{1,0:T(1,128)S(1)}) custom-call(bf16[64,2,512]{2,1,0:T(2,128)(2,1)} %tf_hbm.1, bf16[64,512]{1,0:T(8,128)(2,1)} %bitcast.1, s32[1,64]{1,0:T(1,128)} %pair_hbm.1, bf16[1,64]{1,0:T(2,128)(2,1)} %weight_hbm.1, bf16[512,2048]{1,0:T(8,128)(2,1)} %tp_hbm.1, bf16[512,2048]{1,0:T(8,128)(2,1)} %sp_hbm.1), custom_call_target="tpu_custom_call" | custom-call | tf_op jit(solution)/shard_map/pallas_call | solution.py:439
  65.1 0.7 %shard_map.78 = (f32[1,64,512]{2,1,0:T(8,128)}, f32[1,64]{1,0:T(1,128)}) custom-call(f32[64,512]{1,0:T(8,128)S(1)} %get-tuple-element.4.grad_in, f32[1,64]{1,0:T(1,128)S(1)} %get-tuple-element.5.loss_in), custom_call_target="tpu_custom_call" | custom-call | tf_op jit(solution)/shard_map/pallas_call | solution.py:510

commit v6 on v5

--- a/solution.py
+++ b/solution.py
@@ -54,7 +54,7 @@
     y_n, c_n, z_n,
     tf_hbm, sf_hbm, pair_hbm, weight_hbm, tp_hbm, sp_hbm,
     grad_ref, loss_ref,
-    tf, sf, pair, weight, tp, sp, t_scale, s_scale, t, e, tu, su, part, spart, ubuf, v, csum,
+    tf, sf, pair, weight, tp, sp, t_scale, s_scale, t, e, tu, su, part, spart, ubuf, v, csum, acc,
     r1p, r1z, r2p, r2z, tot_p, tot_sum, tot_z, pairs,
     a_out, a_mid, a_pre, a_in, az_out, az_in, a_all, col_sums,
     ct_out, ct_in, cz_out, cz_in, pick_out, pick_in, r3p, r3z,
@@ -267,11 +267,19 @@
 
     for j in range(2):
         some = slice(j * CHUNK, (j + 1) * CHUNK)
-        back = lax.dot_general(e[...], sp[some, :], NT, preferred_element_type=F32)
-        for c in range(c_n):
-            a_out[c % 2, c // 2, :, some] = back[64 * c : 64 * c + 64, :].astype(BF16)
+        acc[:, some] = lax.dot_general(e[...], sp[some, :], NT, preferred_element_type=F32)
+    for c in range(c_n):
+        rows = slice(64 * c, 64 * c + 64)
+        unit = su[c].astype(F32)
+        product = acc[rows, :] * unit
+        shares = product[:, :LANES]
+        for k in range(1, 4):
+            shares = shares + product[:, k * LANES : (k + 1) * LANES]
+        part[rows, :] = shares
+        alpha = jnp.sum(shares, axis=1, keepdims=True)
+        a_out[c % 2, c // 2] = (acc[rows, :] - alpha * unit).astype(BF16)
     push(a_out.at[1 - side], a_mid, am_s, am_r, "crop", partner)
-    tot_p[my_c] = lane_sums(spart, 4)
+    tot_p[my_c] = jnp.concatenate([lane_sums(spart, 4), lane_sums(part, 4)], axis=0)
     to_crops(lambda peer: tot_p.at[my_c], tot_p.at[my_c], tp_s, tp_r)
     pltpu.make_async_copy(a_mid, a_mid, am_r).wait()
     my_x = my_c // 2
@@ -307,7 +315,7 @@
     await_bytes(tot_p, c_n - 1, tp_r)
     whole = jnp.sum(tot_p[...], axis=0)
     for q in range(4):
-        tot_sum[q] = whole[q : q + 1, :]
+        tot_sum[q] = jnp.concatenate([whole[q : q + 1, :], whole[q + 4 : q + 5, :]], axis=0)
     tot_z[my_z] = tot_sum[my_c // 2]
 
     to_protos(lambda peer: az_out.at[peer], az_in.at[my_z], az_s, az_r)
@@ -334,7 +342,7 @@
 
     await_bytes(az_in, z_n - 1, az_r)
     az_in[my_z] = az_out[my_z]
-    a_all[my_z] = jnp.sum(az_in[...].astype(F32), axis=0)
+    a_all[my_z] = jnp.sum(az_in[...].astype(F32), axis=0).astype(BF16)
     to_protos(lambda peer: a_all.at[my_z], a_all.at[my_z], ag_s, ag_r)
 
     await_bytes(r3p, c_n - 1, r3p_r)
@@ -367,7 +375,9 @@
     await_bytes(pairs, c_n - 1, pr_r)
     views = [as_column(pairs[c], my_c * 8, 8) > 0.5 for c in range(c_n)]
     await_bytes(tot_z, z_n - 1, tz_r)
-    totals = as_column(jnp.sum(tot_z[...], axis=0), side * images, images)
+    both = jnp.sum(tot_z[...], axis=0)
+    totals = as_column(both[0:1, :], side * images, images)
+    alpha = as_column(both[1:2, :], side * images, images)
     await_bytes(r3z, z_n - 1, r3z_r)
     last = 1.0 / jnp.sum(r3z[...], axis=0)
     scales = [as_column(last, images * g + my_c * 8, 8) for g in range(2)]
@@ -394,7 +404,9 @@
     for g in range(8):
         for h in range(2):
             rows = slice(g * 8, g * 8 + 8)
-            grad_ref[rows, h * 256 : (h + 1) * 256] = a_all[2 * g + h] / totals[rows]
+            cols = slice(h * 256, (h + 1) * 256)
+            whole = a_all[2 * g + h].astype(F32) + alpha[rows] * unit[rows, cols]
+            grad_ref[rows, cols] = whole / totals[rows]
     await_bytes(pick_in, 4 * c_n - 1, ca_r)
 
     chosen = jnp.concatenate(
@@ -462,13 +474,14 @@
                 ram((ROWS, LANES), F32),
                 ram((8, COLS), F32),
                 ram((8, COLS), F32),
+                ram((ROWS, ROWS), F32),
                 ram((y_n * c_n, 1, LANES), F32),
                 ram((z_n, 4, LANES), BF16),
                 ram((c_n, 4, LANES), F32),
                 ram((z_n, 4, LANES), BF16),
-                ram((c_n, 4, LANES), F32),
-                ram((4, 1, LANES), F32),
-                ram((z_n, 1, LANES), F32),
+                ram((c_n, 8, LANES), F32),
+                ram((4, 2, LANES), F32),
+                ram((z_n, 2, LANES), F32),
                 ram((c_n, 1, images), F32),
                 ram((2, c_n // 2, images, width), BF16),
                 ram((c_n // 2, images, width), BF16),
@@ -476,7 +489,7 @@
                 ram((c_n // 2, images, width), BF16),
                 ram((z_n, 8, 256), BF16),
                 ram((z_n, 8, 256), BF16),
-                ram((z_n, 8, 256), F32),
+                ram((z_n, 8, 256), BF16),
                 ram((y_n, 1, COLS), F32),
                 ram((c_n, 2, 8, width), BF16),
                 ram((c_n, 2, 8, width), BF16),

time: 65.9 us -> 63.8 us (0.968)
  Pallas kernels: 65.1 us -> 63 us
    pallas_call x1, Pallas kernels: 64.5 us -> 62.4 us  [step(): pl.pallas_call(functools.partial(kernel, y_n, c_n, z_n), out_shape=(jax.S...]
where the time goes in v6:
time: 63.8 us; the launch traced here: 63.7 us
  Pallas kernels  63 us (99%)
  between operations  0.64 us (1%)
    pallas_call x1, Pallas kernels, step(): pl.pallas_call(functools.partial(kernel, y_n, c_n, z_n), out_shape=(jax.S...  62.4 us

profile of v6, /device:TPU:1, one launch (start us, length us, event | category | flops | bytes accessed | tf_op | source)
XLA Modules:
  0.0 63.7 jit_solution(1487541476052952839)
XLA Ops:
  0.6 62.4 %shard_map.77 = (f32[64,512]{1,0:T(8,128)S(1)}, f32[1,64]{1,0:T(1,128)S(1)}) custom-call(bf16[64,2,512]{2,1,0:T(2,128)(2,1)} %tf_hbm.1, bf16[64,512]{1,0:T(8,128)(2,1)} %bitcast.1, s32[1,64]{1,0:T(1,128)} %pair_hbm.1, bf16[1,64]{1,0:T(2,128)(2,1)} %weight_hbm.1, bf16[512,2048]{1,0:T(8,128)(2,1)} %tp_hbm.1, bf16[512,2048]{1,0:T(8,128)(2,1)} %sp_hbm.1), custom_call_target="tpu_custom_call" | custom-call | tf_op jit(solution)/shard_map/pallas_call | solution.py:451
  63.0 0.7 %shard_map.78 = (f32[1,64,512]{2,1,0:T(8,128)}, f32[1,64]{1,0:T(1,128)}) custom-call(f32[64,512]{1,0:T(8,128)S(1)} %get-tuple-element.4.grad_in, f32[1,64]{1,0:T(1,128)S(1)} %get-tuple-element.5.loss_in), custom_call_target="tpu_custom_call" | custom-call | tf_op jit(solution)/shard_map/pallas_call | solution.py:523

commit v7 on v6

--- a/solution.py
+++ b/solution.py
@@ -194,7 +194,7 @@
             part[pl.ds(pl.multiple_of(r * 8, 8), 8), :] = total
             return carry
 
-        lax.fori_loop(0, n // 8, block, 0, unroll=4)
+        lax.fori_loop(0, n // 8, block, 0, unroll=8)
         return lane_sums(part, n // LANES)
 
     def column_pass(row_sums):
@@ -210,7 +210,7 @@
             )
 
         zero = tuple(jnp.zeros((8, LANES), F32) for _ in range(COLS // LANES))
-        set_v(lax.fori_loop(0, ROWS // 8, block, zero, unroll=4))
+        set_v(lax.fori_loop(0, ROWS // 8, block, zero, unroll=8))
 
     await_bytes(col_sums, y_n - 1, cs_r)
     v[...] = jnp.broadcast_to(1.0 / jnp.sum(col_sums[...], axis=0), (8, COLS))
@@ -277,7 +277,9 @@
             shares = shares + product[:, k * LANES : (k + 1) * LANES]
         part[rows, :] = shares
         alpha = jnp.sum(shares, axis=1, keepdims=True)
-        a_out[c % 2, c // 2] = (acc[rows, :] - alpha * unit).astype(BF16)
+        rest = acc[rows, :] - alpha * unit
+        acc[rows, :] = rest
+        a_out[c % 2, c // 2] = rest.astype(BF16)
     push(a_out.at[1 - side], a_mid, am_s, am_r, "crop", partner)
     tot_p[my_c] = jnp.concatenate([lane_sums(spart, 4), lane_sums(part, 4)], axis=0)
     to_crops(lambda peer: tot_p.at[my_c], tot_p.at[my_c], tp_s, tp_r)
@@ -285,7 +287,8 @@
     my_x = my_c // 2
 
     def merge(x):
-        a_pre[x] = (a_out[side, x].astype(F32) + a_mid[x].astype(F32)).astype(BF16)
+        rows = pl.ds(pl.multiple_of((2 * x + side) * 64, 64), 64)
+        a_pre[x] = (acc[rows, :] + a_mid[x].astype(F32)).astype(BF16)
 
     every(c_n // 2, merge)
 
@@ -331,13 +334,13 @@
         e[0:LANES, cols] = (scaled * s_scale[0:1, cols]).astype(BF16)
         halves = scaled[:, :LANES] + scaled[:, LANES:]
         part[0:LANES, :] = halves if k == 0 else part[0:LANES, :] + halves
-    r3p[my_c] = lane_sums(part, 1)
-    to_crops(lambda peer: r3p.at[my_c], r3p.at[my_c], r3p_s, r3p_r)
     sums = lax.dot_general(e[0:LANES, :], sp[...], NT, preferred_element_type=F32)
     for c in range(c_n):
         for g in range(2):
             ct_out[c, g] = sums[64 * g + 8 * c : 64 * g + 8 * c + 8, :].astype(BF16)
     to_crops(lambda peer: ct_out.at[peer], ct_in.at[my_c], ct_s, ct_r)
+    r3p[my_c] = lane_sums(part, 1)
+    to_crops(lambda peer: r3p.at[my_c], r3p.at[my_c], r3p_s, r3p_r)
     ct_in[my_c] = ct_out[my_c]
 
     await_bytes(az_in, z_n - 1, az_r)
@@ -345,9 +348,6 @@
     a_all[my_z] = jnp.sum(az_in[...].astype(F32), axis=0).astype(BF16)
     to_protos(lambda peer: a_all.at[my_z], a_all.at[my_z], ag_s, ag_r)
 
-    await_bytes(r3p, c_n - 1, r3p_r)
-    r3z[my_z] = jnp.sum(r3p[...], axis=0)
-    to_protos(lambda peer: r3z.at[my_z], r3z.at[my_z], r3z_s, r3z_r)
     await_bytes(ct_in, c_n - 1, ct_r)
     total = jnp.sum(ct_in[...].astype(F32), axis=0)
     mine = lax.rem(my_z, 4)
@@ -355,6 +355,9 @@
         tile = total[:, :, k * LANES : (k + 1) * LANES].reshape(16, LANES)
         cz_out[k] = tile.astype(BF16)
     to_protos(lambda peer: cz_out.at[lax.rem(peer, 4)], cz_in.at[my_z], cz_s, cz_r)
+    await_bytes(r3p, c_n - 1, r3p_r)
+    r3z[my_z] = jnp.sum(r3p[...], axis=0)
+    to_protos(lambda peer: r3z.at[my_z], r3z.at[my_z], r3z_s, r3z_r)
     cz_in[my_z] = cz_out[mine]
 
     images = ROWS // c_n

time: 63.8 us -> 65.2 us (1.022)
  Pallas kernels: 63 us -> 64.4 us
    pallas_call x1, Pallas kernels: 62.4 us -> 63.8 us  [step(): pl.pallas_call(functools.partial(kernel, y_n, c_n, z_n), out_shape=(jax.S...]
where the time goes in v7:
time: 65.2 us; the launch traced here: 65.1 us
  Pallas kernels  64.4 us (99%)
    pallas_call x1, Pallas kernels, step(): pl.pallas_call(functools.partial(kernel, y_n, c_n, z_n), out_shape=(jax.S...  63.8 us

profile of v7, /device:TPU:1, one launch (start us, length us, event | category | flops | bytes accessed | tf_op | source)
XLA Modules:
  0.0 65.1 jit_solution(6756680961630013193)
XLA Ops:
  0.6 63.8 %shard_map.77 = (f32[64,512]{1,0:T(8,128)S(1)}, f32[1,64]{1,0:T(1,128)S(1)}) custom-call(bf16[64,2,512]{2,1,0:T(2,128)(2,1)} %tf_hbm.1, bf16[64,512]{1,0:T(8,128)(2,1)} %bitcast.1, s32[1,64]{1,0:T(1,128)} %pair_hbm.1, bf16[1,64]{1,0:T(2,128)(2,1)} %weight_hbm.1, bf16[512,2048]{1,0:T(8,128)(2,1)} %tp_hbm.1, bf16[512,2048]{1,0:T(8,128)(2,1)} %sp_hbm.1), custom_call_target="tpu_custom_call" | custom-call | tf_op jit(solution)/shard_map/pallas_call | solution.py:454
  64.4 0.7 %shard_map.78 = (f32[1,64,512]{2,1,0:T(8,128)}, f32[1,64]{1,0:T(1,128)}) custom-call(f32[64,512]{1,0:T(8,128)S(1)} %get-tuple-element.4.grad_in, f32[1,64]{1,0:T(1,128)S(1)} %get-tuple-element.5.loss_in), custom_call_target="tpu_custom_call" | custom-call | tf_op jit(solution)/shard_map/pallas_call | solution.py:526

commit v8 on v6

--- a/solution.py
+++ b/solution.py
@@ -22,7 +22,8 @@
 
 
 def every(n, body):
-    lax.fori_loop(0, n, lambda k, c: (body(k), c)[1], 0)
+    unroll = next(u for u in (31, 7, 5, 3, 1) if n % u == 0) if n > 2 else 1
+    lax.fori_loop(0, n, lambda k, c: (body(k), c)[1], 0, unroll=unroll)
 
 
 def unit_rows(x):

time: 63.8 us -> 62.8 us (0.984)
  Pallas kernels: 63 us -> 62 us
    pallas_call x1, Pallas kernels: 62.4 us -> 61.4 us  [step(): pl.pallas_call(functools.partial(kernel, y_n, c_n, z_n), out_shape=(jax.S...]
where the time goes in v8:
time: 62.8 us; the launch traced here: 62.7 us
  Pallas kernels  62 us (99%)
  between operations  0.64 us (1%)
    pallas_call x1, Pallas kernels, step(): pl.pallas_call(functools.partial(kernel, y_n, c_n, z_n), out_shape=(jax.S...  61.4 us

profile of v8, /device:TPU:1, one launch (start us, length us, event | category | flops | bytes accessed | tf_op | source)
XLA Modules:
  0.0 62.7 jit_solution(15407966615423231854)
XLA Ops:
  0.6 61.4 %shard_map.77 = (f32[64,512]{1,0:T(8,128)S(1)}, f32[1,64]{1,0:T(1,128)S(1)}) custom-call(bf16[64,2,512]{2,1,0:T(2,128)(2,1)} %tf_hbm.1, bf16[64,512]{1,0:T(8,128)(2,1)} %bitcast.1, s32[1,64]{1,0:T(1,128)} %pair_hbm.1, bf16[1,64]{1,0:T(2,128)(2,1)} %weight_hbm.1, bf16[512,2048]{1,0:T(8,128)(2,1)} %tp_hbm.1, bf16[512,2048]{1,0:T(8,128)(2,1)} %sp_hbm.1), custom_call_target="tpu_custom_call" | custom-call | tf_op jit(solution)/shard_map/pallas_call | solution.py:452
  62.0 0.7 %shard_map.78 = (f32[1,64,512]{2,1,0:T(8,128)}, f32[1,64]{1,0:T(1,128)}) custom-call(f32[64,512]{1,0:T(8,128)S(1)} %get-tuple-element.4.grad_in, f32[1,64]{1,0:T(1,128)S(1)} %get-tuple-element.5.loss_in), custom_call_target="tpu_custom_call" | custom-call | tf_op jit(solution)/shard_map/pallas_call | solution.py:524
